TPU v7x, 128 devices: a whole 4x4x4 slice. The times are simulated.
128 devices in a mesh: dp: 1, tp: 16 (over z, y), cp: 8 (over x, core).
Axes of the slice: x: 4, y: 4, z: 4, core: 2. Of those that a mesh axis runs over, the one named last changes fastest.
Arguments:
- x_in: bfloat16 [8192, 4096], P(('dp', 'cp', 'tp'))
- w_query: bfloat16 [4096, 32, 128], P(None, 'tp')
- w_key: bfloat16 [4096, 32, 128], P(None, 'tp')
- w_value: bfloat16 [4096, 32, 128], P(None, 'tp')
- w_out: bfloat16 [32, 128, 4096], P('tp')
- d_out: bfloat16 [8192, 4096], P(('dp', 'cp', 'tp'))
Outputs:
- output 1: bfloat16 [8192, 4096], P(('dp', 'cp', 'tp'))
- output 2: bfloat16 [8192, 4096], P(('dp', 'cp', 'tp'))
- output 3: bfloat16 [8, 4096, 32, 128], P(('dp', 'cp'), None, 'tp')
- output 4: bfloat16 [8, 4096, 32, 128], P(('dp', 'cp'), None, 'tp')
- output 5: bfloat16 [8, 4096, 32, 128], P(('dp', 'cp'), None, 'tp')
- output 6: bfloat16 [8, 32, 128, 4096], P(('dp', 'cp'), 'tp')
All inputs are finite; a program needn't handle non-finite values.
Results may differ from a plain program's by a relative error of at most 0.00935223.
Values are sent between devices in bfloat16 or wider.
A program may use at most 1 GiB of HBM per device.

v0:
```python
import functools
import math

import jax
import jax.numpy as jnp
from jax import lax
from jax.experimental import pallas as pl
from jax.experimental.pallas import tpu as pltpu
from jax.sharding import PartitionSpec as P

ROW_SPEC = P(("dp", "cp", "tp"), None)
HEAD_SPEC = P(None, "tp", None)
OUT_W_SPEC = P("tp", None, None)
GRAD_SPEC = P(("dp", "cp"), None, "tp", None)
GRAD_OUT_SPEC = P(("dp", "cp"), "tp", None, None)
COLS_CONTRACT = (((1,), (1,)), ((), ()))
ROWS_CONTRACT = (((0,), (0,)), ((), ()))
VMEM_LIMIT = 58 * 1024 * 1024
F32 = jnp.float32
BF16 = jnp.bfloat16


def dot_t(lhs, rhs):
    return lax.dot_general(lhs, rhs, COLS_CONTRACT, preferred_element_type=F32)


def dot_n(lhs, rhs):
    return jnp.dot(lhs, rhs, preferred_element_type=F32)


def block_slot(pos_blk, n_sh):
    return jnp.where(pos_blk < n_sh, 2 * pos_blk, 2 * (2 * n_sh - 1 - pos_blk) + 1)


def shard_exchange(n_sh, pairs, sends, recvs):
    n_x = n_sh // 2
    rank = lax.axis_index("cp")
    chip, core = rank // 2, lax.rem(rank, 2)

    def rank_of(dx, dc):
        return 2 * lax.rem(chip + dx, n_x) + lax.rem(core + dc, 2)

    n_kinds = 9
    kinds = {"prev": 0, "next": 1, "far_lo": 2, "far_hi": 3, "own_x": 4, "prev_x": 5, "next_x": 6, "far_lo_x": 7, "far_hi_x": 8}

    def part(buf, dx, dc, half):
        return buf.at[pl.ds(2 * rank_of(dx, dc) + (0 if half is None else half), 2 if half is None else 1)]

    routes = {
        "prev": ((0, 0), None, (1, 0)), "next": ((0, 0), None, (n_x - 1, 0)), "own_x": ((0, 0), None, (0, 1)),
        "far_lo": ((n_x - 1, 0), 0, (1, 0)), "far_hi": ((1, 0), 1, (n_x - 1, 0)),
        "prev_x": ((n_x - 1, 0), None, (0, 1)), "next_x": ((1, 0), None, (0, 1)),
        "far_lo_x": ((2, 0), 0, (0, 1)), "far_hi_x": ((2, 0), 1, (0, 1)),
    }

    def copies(kind):
        (dx, dc), half, target = routes[kind]
        out = []
        for idx, (own, buf) in enumerate(pairs):
            dst = part(buf, dx, dc, half)
            src = own if (dx, dc) == (0, 0) else dst
            out.append(pltpu.make_async_remote_copy(
                src_ref=src, dst_ref=dst, send_sem=sends.at[idx * n_kinds + kinds[kind]], recv_sem=recvs.at[idx * n_kinds + kinds[kind]],
                device_id={"cp": rank_of(*target)}, device_id_type=pl.DeviceIdType.MESH))
        return out

    def start(*names):
        for name in names:
            for copy in copies(name):
                copy.start()

    def wait_recv(*names):
        for name in names:
            for copy in copies(name):
                copy.wait_recv()

    def wait_sends():
        for name in routes:
            for copy in copies(name):
                copy.wait_send()

    def barrier():
        sem = pltpu.get_barrier_semaphore()
        for target in ((1, 0), (n_x - 1, 0), (0, 1)):
            pl.semaphore_signal(sem, inc=1, device_id={"cp": rank_of(*target)}, device_id_type=pl.DeviceIdType.MESH)
        pl.semaphore_wait(sem, 3)

    return rank, rank_of, barrier, start, wait_recv, wait_sends


def causal_mask(rows, cols, transposed=False):
    row_ids = lax.broadcasted_iota(jnp.int32, (rows, cols), 0)
    col_ids = lax.broadcasted_iota(jnp.int32, (rows, cols), 1)
    return col_ids >= row_ids if transposed else row_ids >= col_ids


def forward_kernel(n_sh, heads, dim, q_ref, kv_ref, o_ref, lse_ref, all_ref, kv_buf, m_ref, l_ref, acc_ref, sends, recvs, sems):
    rank, rank_of, barrier, start, wait_recv, wait_sends = shard_exchange(n_sh, [(kv_ref, kv_buf)], sends, recvs)
    n_x = n_sh // 2
    barrier()
    start("prev", "next", "own_x")
    width = heads * dim
    half_rows = q_ref.shape[1]
    log2e_scale = math.log2(math.e) * dim ** -0.5
    own = pltpu.make_async_copy(kv_ref, kv_buf.at[pl.ds(2 * rank, 2)], sems.at[0])
    own.start()
    own.wait()
    for half in range(2):
        for h in range(heads):
            cols = slice(h * dim, (h + 1) * dim)
            vcols = slice(width + h * dim, width + (h + 1) * dim)
            k_blk = kv_buf[2 * rank + half, :, cols]
            v_blk = kv_buf[2 * rank + half, :, vcols]
            s = dot_t(q_ref[half, :, cols], k_blk)
            s = jnp.where(causal_mask(half_rows, half_rows), s, -jnp.inf)
            m = jnp.max(s, axis=1, keepdims=True)
            p = jnp.exp2((s - m) * log2e_scale)
            m_ref[half, h] = jnp.broadcast_to(m, (half_rows, dim))
            l_ref[half, h] = jnp.broadcast_to(jnp.sum(p, axis=1, keepdims=True), (half_rows, dim))
            acc_ref[half, h] = dot_n(p.astype(BF16), v_blk)

    def unit(late, slot):
        for h in range(heads):
            cols = slice(h * dim, (h + 1) * dim)
            vcols = slice(width + h * dim, width + (h + 1) * dim)
            k_blk = kv_buf[slot, :, cols]
            v_blk = kv_buf[slot, :, vcols]
            s = dot_t(q_ref[late, :, cols], k_blk)
            m_old = m_ref[late, h]
            m_new = jnp.maximum(m_old, jnp.max(s, axis=1, keepdims=True))
            factor = jnp.exp2((m_old - m_new) * log2e_scale)
            p = jnp.exp2((s - m_new[:, :1]) * log2e_scale)
            m_ref[late, h] = m_new
            l_ref[late, h] = l_ref[late, h] * factor + jnp.sum(p, axis=1, keepdims=True)
            acc_ref[late, h] = acc_ref[late, h] * factor + dot_n(p.astype(BF16), v_blk)

    def visit(first, count, shard_of):
        def step(t, carry):
            shard = shard_of(t // 2)
            after = (shard > rank).astype(jnp.int32)
            second = lax.rem(t, 2)
            late = jnp.where(second == 1, after, 1)
            slot = 2 * shard + jnp.where(second == 1, after, 0)
            unit(late, slot)
            return carry
        lax.fori_loop(first, first + count, step, 0)

    offsets = [(0, 0), (0, 1), (n_x - 1, 0), (1, 0), (n_x - 1, 1), (1, 1), (2, 0), (2, 1)]

    def shard_of(idx):
        out = rank_of(*offsets[0])
        for pos in range(1, n_sh):
            out = jnp.where(idx == pos, rank_of(*offsets[pos]), out)
        return out

    visit(0, 1, shard_of)
    wait_recv("own_x")
    visit(2, 2, shard_of)
    wait_recv("prev")
    start("far_lo", "prev_x")
    wait_recv("next")
    start("far_hi", "next_x")
    visit(4, 4, shard_of)
    wait_recv("prev_x", "next_x")
    visit(8, 2, shard_of)
    wait_recv("far_lo", "far_hi")
    start("far_lo_x", "far_hi_x")
    visit(10, 4, shard_of)
    wait_recv("far_lo_x", "far_hi_x")
    out = pltpu.make_async_copy(kv_buf, all_ref, sems.at[0])
    out.start()
    visit(14, 2, shard_of)
    for half in range(2):
        for h in range(heads):
            cols = slice(h * dim, (h + 1) * dim)
            l = l_ref[half, h]
            o_ref[half, :, cols] = (acc_ref[half, h] / l).astype(BF16)
            lse = m_ref[half, h] * log2e_scale + jnp.log2(l)
            lse_ref[half, h:h + 1, :] = jnp.transpose(lse)[:1]
    out.wait()
    wait_sends()


def stats_kernel(heads, dim, o_ref, do_ref, lse_ref, out_ref):
    half_rows = o_ref.shape[1]
    for half in range(2):
        rows = [lse_ref[half]]
        for h in range(heads):
            cols = slice(h * dim, (h + 1) * dim)
            prod = do_ref[half, :, cols].astype(F32) * o_ref[half, :, cols].astype(F32)
            delta = jnp.broadcast_to(jnp.sum(prod, axis=1, keepdims=True), (half_rows, dim))
            rows.append(jnp.transpose(delta)[:1])
        rows.append(jnp.zeros((8 - 2 * heads, half_rows), F32))
        out_ref[half] = jnp.concatenate(rows, axis=0)


def backward_kernel(n_sh, heads, dim, q_ref, do_ref, st_ref, all_ref, dq_ref, dkv_ref,
                    kv_buf, q_buf, do_buf, st_buf, acc_ref, lse_ref, dot_ref, dk_acc, dv_acc, sends, recvs, sems):
    rank, rank_of, barrier, start, wait_recv, wait_sends = shard_exchange(
        n_sh, [(q_ref, q_buf), (do_ref, do_buf), (st_ref, st_buf)], sends, recvs)
    n_x = n_sh // 2
    barrier()
    start("prev", "next", "own_x")
    load = [pltpu.make_async_copy(all_ref, kv_buf, sems.at[0])]
    for idx, (own, buf) in enumerate([(q_ref, q_buf), (do_ref, do_buf), (st_ref, st_buf)]):
        load.append(pltpu.make_async_copy(own, buf.at[pl.ds(2 * rank, 2)], sems.at[1 + idx]))
    for copy in load:
        copy.start()
    width = heads * dim
    half_rows = q_ref.shape[1]
    scale = dim ** -0.5
    log2e_scale = math.log2(math.e) * scale
    for half in range(2):
        for h in range(heads):
            lse_ref[half, h] = jnp.transpose(jnp.broadcast_to(st_ref[half, h:h + 1, :], (dim, half_rows)))
            dot_ref[half, h] = jnp.transpose(jnp.broadcast_to(st_ref[half, heads + h:heads + h + 1, :], (dim, half_rows)))
    for copy in load:
        copy.wait()

    def query_part(half, slot, h, masked):
        cols = slice(h * dim, (h + 1) * dim)
        vcols = slice(width + h * dim, width + (h + 1) * dim)
        k_blk = kv_buf[slot, :, cols]
        v_blk = kv_buf[slot, :, vcols]
        s = dot_t(q_ref[half, :, cols], k_blk)
        p = jnp.exp2(s * log2e_scale - lse_ref[half, h][:, :1])
        if masked:
            p = jnp.where(causal_mask(half_rows, half_rows), p, 0.0)
        dp = dot_t(do_ref[half, :, cols], v_blk)
        ds = (p * (dp - dot_ref[half, h][:, :1])).astype(BF16)
        return dot_n(ds, k_blk)

    for half in range(2):
        for h in range(heads):
            acc_ref[half, h] = query_part(half, 2 * rank + half, h, True)

    def query_step(t, carry):
        late = (t >= rank).astype(jnp.int32)
        slot = block_slot(t - late * rank, n_sh)
        for h in range(heads):
            acc_ref[late, h] = acc_ref[late, h] + query_part(late, slot, h, False)
        return carry

    lax.fori_loop(0, 2 * n_sh - 1, query_step, 0)
    wait_recv("prev")
    start("far_lo", "prev_x")
    wait_recv("next")
    start("far_hi", "next_x")
    for half in range(2):
        for h in range(heads):
            dq_ref[half, :, h * dim:(h + 1) * dim] = (acc_ref[half, h] * scale).astype(BF16)

    def key_part(half, slot, h, masked):
        cols = slice(h * dim, (h + 1) * dim)
        vcols = slice(width + h * dim, width + (h + 1) * dim)
        q_blk = q_buf[slot, :, cols]
        do_blk = do_buf[slot, :, cols]
        k_slot = 2 * rank + half
        s = dot_t(kv_buf[k_slot, :, cols], q_blk)
        p = jnp.exp2(s * log2e_scale - st_buf[slot, h:h + 1, :])
        if masked:
            p = jnp.where(causal_mask(half_rows, half_rows, transposed=True), p, 0.0)
        dp = dot_t(kv_buf[k_slot, :, vcols], do_blk)
        ds = (p * (dp - st_buf[slot, heads + h:heads + h + 1, :])).astype(BF16)
        return dot_n(ds, q_blk), dot_n(p.astype(BF16), do_blk)

    for half in range(2):
        for h in range(heads):
            dk_acc[half, h], dv_acc[half, h] = key_part(half, 2 * rank + half, h, True)

    offsets = [(0, 0), (0, 1), (n_x - 1, 0), (1, 0), (n_x - 1, 1), (1, 1), (2, 0), (2, 1)]

    def visit(first, count):
        def step(t, carry):
            idx = t // 2
            shard = rank_of(*offsets[0])
            for pos in range(1, n_sh):
                shard = jnp.where(idx == pos, rank_of(*offsets[pos]), shard)
            before = (shard < rank).astype(jnp.int32)
            second = lax.rem(t, 2)
            late = jnp.where(second == 1, before, 0)
            slot = 2 * shard + jnp.where(second == 1, before, 1)
            for h in range(heads):
                dk_part, dv_part = key_part(late, slot, h, False)
                dk_acc[late, h] = dk_acc[late, h] + dk_part
                dv_acc[late, h] = dv_acc[late, h] + dv_part
            return carry
        lax.fori_loop(first, first + count, step, 0)

    visit(0, 1)
    wait_recv("own_x")
    visit(2, 6)
    wait_recv("prev_x", "next_x")
    visit(8, 2)
    wait_recv("far_lo", "far_hi")
    start("far_lo_x", "far_hi_x")
    visit(10, 4)
    wait_recv("far_lo_x", "far_hi_x")
    visit(14, 2)
    for half in range(2):
        for h in range(heads):
            cols = slice(h * dim, (h + 1) * dim)
            vcols = slice(width + h * dim, width + (h + 1) * dim)
            dkv_ref[half, :, cols] = (dk_acc[half, h] * scale).astype(BF16)
            dkv_ref[half, :, vcols] = dv_acc[half, h].astype(BF16)
    wait_sends()


VMEM_SPEC = pl.BlockSpec(memory_space=pltpu.VMEM)
ANY_SPEC = pl.BlockSpec(memory_space=pl.ANY)


def attention_call(kernel, name, collective_id, flops, in_specs, out_specs, out_shape, scratch):
    return pl.pallas_call(
        kernel,
        name=name,
        out_shape=out_shape,
        in_specs=in_specs,
        out_specs=out_specs,
        scratch_shapes=scratch,
        cost_estimate=pl.CostEstimate(flops=flops, bytes_accessed=10 * 2 ** 20, transcendentals=0),
        compiler_params=pltpu.CompilerParams(vmem_limit_bytes=VMEM_LIMIT, collective_id=collective_id, has_side_effects=True),
    )


def solution(mesh):
    n_sh = mesh.shape["cp"]

    def device_fn(x_blk, w_query, w_key, w_value, w_out, dy_blk):
        model_dim, heads, dim = w_query.shape
        width = heads * dim
        wq = w_query.reshape(model_dim, width)
        wkv = jnp.concatenate([w_key.reshape(model_dim, width), w_value.reshape(model_dim, width)], axis=1)
        wo = w_out.reshape(width, model_dim)

        x_rows = lax.all_gather(x_blk, "tp", axis=0, tiled=True)
        dy_rows = lax.all_gather(dy_blk, "tp", axis=0, tiled=True)
        n_rows = x_rows.shape[0]
        half_rows = n_rows // 2
        tile_flops = 4 * (2 * n_sh + 1) * half_rows * half_rows * heads * dim

        kv = dot_n(x_rows, wkv).astype(BF16).reshape(2, half_rows, 2 * width)
        q = dot_n(x_rows, wq).astype(BF16).reshape(2, half_rows, width)
        acc = pltpu.VMEM((2, heads, half_rows, dim), F32)
        dma = pltpu.SemaphoreType.DMA
        kv_all_shape = (2 * n_sh, half_rows, 2 * width)

        o, lse, kv_all = attention_call(
            functools.partial(forward_kernel, n_sh, heads, dim), "attn_fwd", 0, 2 * tile_flops,
            [VMEM_SPEC, VMEM_SPEC], [VMEM_SPEC, VMEM_SPEC, ANY_SPEC],
            [jax.ShapeDtypeStruct((2, half_rows, width), BF16), jax.ShapeDtypeStruct((2, heads, half_rows), F32),
             jax.ShapeDtypeStruct(kv_all_shape, BF16)],
            [pltpu.VMEM(kv_all_shape, BF16), acc, acc, acc, dma((9,)), dma((9,)), dma((1,))],
        )(q, kv)
        o_flat = o.reshape(n_rows, width)
        y_part = dot_n(o_flat, wo)
        y_blk = lax.psum_scatter(y_part, "tp", scatter_dimension=0, tiled=True).astype(BF16)

        d_o = dot_t(dy_rows, wo).astype(BF16).reshape(2, half_rows, width)
        stats = pl.pallas_call(
            functools.partial(stats_kernel, heads, dim),
            name="attn_stats",
            out_shape=jax.ShapeDtypeStruct((2, 8, half_rows), F32),
        )(o, d_o, lse)
        shard_buf = pltpu.VMEM((2 * n_sh, half_rows, width), BF16)
        dq, dkv = attention_call(
            functools.partial(backward_kernel, n_sh, heads, dim), "attn_bwd", 1, 7 * tile_flops // 2,
            [VMEM_SPEC, VMEM_SPEC, VMEM_SPEC, ANY_SPEC], [VMEM_SPEC, VMEM_SPEC],
            [jax.ShapeDtypeStruct((2, half_rows, width), BF16), jax.ShapeDtypeStruct((2, half_rows, 2 * width), BF16)],
            [pltpu.VMEM(kv_all_shape, BF16), shard_buf, shard_buf, pltpu.VMEM((2 * n_sh, 8, half_rows), F32),
             acc, acc, acc, acc, acc, dma((27,)), dma((27,)), dma((4,))],
        )(q, d_o, stats, kv_all)

        dq_flat = dq.reshape(n_rows, width)
        dkv_flat = dkv.reshape(n_rows, 2 * width)
        d_all = jnp.concatenate([dq_flat, dkv_flat], axis=1)
        w_all = jnp.concatenate([wq, wkv], axis=1)
        dx_part = dot_t(d_all, w_all)
        dx_blk = lax.psum_scatter(dx_part, "tp", scatter_dimension=0, tiled=True).astype(BF16)

        def weight_grad(lhs, rhs, shape):
            return lax.dot_general(lhs, rhs, ROWS_CONTRACT, preferred_element_type=F32).astype(BF16).reshape(shape)[None]

        grad_wo = weight_grad(o_flat, dy_rows, (heads, dim, model_dim))
        grad_wq = weight_grad(x_rows, dq_flat, (model_dim, heads, dim))
        grad_wk = weight_grad(x_rows, dkv_flat[:, :width], (model_dim, heads, dim))
        grad_wv = weight_grad(x_rows, dkv_flat[:, width:], (model_dim, heads, dim))
        return y_blk, dx_blk, grad_wq, grad_wk, grad_wv, grad_wo

    return jax.shard_map(device_fn, mesh=mesh,
                         in_specs=(ROW_SPEC, HEAD_SPEC, HEAD_SPEC, HEAD_SPEC, OUT_W_SPEC, ROW_SPEC),
                         out_specs=(ROW_SPEC, ROW_SPEC, GRAD_SPEC, GRAD_SPEC, GRAD_SPEC, GRAD_OUT_SPEC),
                         check_vma=False)
```

profile of v0, /device:TPU:0, one launch (start us, length us, event | category | flops | bytes accessed | tf_op | source)
XLA Modules:
  0.0 461.4 jit_solution(5406927440426701389)
XLA Ops:
  8.7 3.3 copy.23
  12.1 2.9 copy_bitcast_fusion
  14.9 68.5 %all-gather.3.cloned.1.call-done = bf16[1024,4096]{1,0:T(8,128)(2,1)} async-done(((bf16[64,4096]{1,0:T(8,128)(2,1)}), bf16[1024,4096]{1,0:T(8,128)(2,1)}) %all-gather.3.cloned.1.call-update) | async-done | bytes 8388624 | tf_op jit(solution)/shard_map/all_gather | solution.py:336
  83.4 9.2 %fusion.16 = bf16[1024,512]{0,1:T(8,128)(2,1)S(1)} fusion(bf16[1024,4096]{1,0:T(8,128)(2,1)} %all-gather.3.cloned.1.call-done, bf16[4096,256]{1,0:T(8,128)(2,1)} %get-tuple-element.22, bf16[4096,256]{1,0:T(8,128)(2,1)} %get-tuple-element.23), kind=kOutput, calls=%fused_computation.21 | convolution fusion | flops 4303880192 | bytes 13631488 | tf_op jit(solution)/shard_map/dot_general | solution.py:28
  92.6 1.5 copy.12
  94.1 7.1 %convolution_convert_fusion.5 = bf16[1024,256]{1,0:T(8,128)(2,1)} fusion(bf16[1024,4096]{1,0:T(8,128)(2,1)} %all-gather.3.cloned.1.call-done, bf16[512,8,2,128]{3,2,1,0:T(2,128)(2,1)} %bitcast.54), kind=kOutput, calls=%fused_computation.23 | convolution fusion | flops 2147745792 | bytes 11010048 | tf_op jit(solution)/shard_map/dot_general | solution.py:28
  101.2 50.7 %attn_fwd.1 = (bf16[2,512,256]{2,1,0:T(8,128)(2,1)}, f32[2,2,512]{2,1,0:T(2,128)}, bf16[16,512,512]{2,1,0:T(8,128)(2,1)}) custom-call(bf16[2,512,256]{2,1,0:T(8,128)(2,1)} %bitcast.63, bf16[2,512,512]{2,1,0:T(8,128)(2,1)} %bitcast.58), custom_call_target="tpu_custom_call" | custom-call | flops 9126805504 | bytes 10485760 | tf_op jit(solution)/shard_map/attn_fwd/pallas_call | solution.py:348
  151.9 4.0 all-gather.5.cloned.1.call-done
  155.9 6.5 %convolution_convert_fusion.4 = bf16[1024,256]{1,0:T(8,128)(2,1)} fusion(bf16[1024,4096]{1,0:T(8,128)(2,1)} %all-gather.5.cloned.1.call-done, bf16[256,4096]{1,0:T(8,128)(2,1)S(1)} %bitcast.43), kind=kOutput, calls=%fused_computation.22 | convolution fusion | flops 2147745792 | bytes 11010048 | tf_op jit(solution)/shard_map/dot_general | solution.py:24
  162.4 2.4 attn_stats.1.st_ref
  164.9 52.5 %attn_bwd.1 = (bf16[2,512,256]{2,1,0:T(8,128)(2,1)}, bf16[2,512,512]{2,1,0:T(8,128)(2,1)}) custom-call(bf16[2,512,256]{2,1,0:T(8,128)(2,1)} %bitcast.64, bf16[2,512,256]{2,1,0:T(8,128)(2,1)} %bitcast.62, f32[2,8,512]{2,1,0:T(8,128)} %attn_stats.1.st_ref, bf16[16,512,512]{2,1,0:T(8,128)(2,1)} %get-tuple-element.13.all_ref), custom_call_target="tpu_custom_call" | custom-call | flops 15971909632 | bytes 10485760 | tf_op jit(solution)/shard_map/attn_bwd/pallas_call | solution.py:366
  217.4 12.2 %fusion = f32[1024,4096]{1,0:T(8,128)} fusion(bf16[4096,256]{1,0:T(8,128)(2,1)} %get-tuple-element.22, bf16[4096,256]{1,0:T(8,128)(2,1)} %get-tuple-element.23, bf16[4096,256]{1,0:T(8,128)(2,1)S(1)} %bitcast.55, bf16[1024,512]{1,0:T(8,128)(2,1)} %bitcast.49, bf16[1024,256]{1,0:T(8,128)(2,1)} %bitcast.59), kind=kOutput, calls=%fused_computation | convolution fusion | flops 6464471040 | bytes 24641536 | tf_op jit(solution)/shard_map/dot_general | solution.py:24
  230.6 8.1 %fusion.23 = f32[1024,4096]{1,0:T(8,128)} fusion(bf16[1024,256]{1,0:T(8,128)(2,1)S(1)} %bitcast.47, bf16[256,4096]{1,0:T(8,128)(2,1)S(1)} %bitcast.42), kind=kOutput, calls=%fused_computation.28 | convolution fusion | flops 2147483648 | bytes 19398656 | tf_op jit(solution)/shard_map/dot_general | solution.py:28
  239.7 7.1 %convolution_convert_fusion.3 = bf16[256,4096]{1,0:T(8,128)(2,1)} fusion(bf16[1024,256]{1,0:T(8,128)(2,1)S(1)} %bitcast.60, bf16[1024,4096]{1,0:T(8,128)(2,1)} %all-gather.3.cloned.1.call-done), kind=kOutput, calls=%fused_computation.9 | convolution fusion | flops 2148532224 | bytes 11010048 | tf_op jit(solution)/shard_map/dot_general | solution.py:382
  246.8 6.3 %copy.13 = bf16[1,4096,2,128]{3,2,1,0:T(2,128)(2,1)} copy(bf16[1,4096,2,128]{1,3,2,0:T(8,128)(2,1)} %bitcast.44) | data formatting | bytes 4194304
  253.1 7.3 %convolution_convert_fusion.2 = bf16[256,4096]{1,0:T(8,128)(2,1)} fusion(bf16[1024,4096]{1,0:T(8,128)(2,1)} %all-gather.3.cloned.1.call-done, bf16[1024,512]{1,0:T(8,128)(2,1)} %bitcast.50), kind=kOutput, calls=%fused_computation.8 | convolution fusion | flops 2148532224 | bytes 11010048 | tf_op jit(solution)/shard_map/dot_general | solution.py:382
  260.4 6.2 %copy.14 = bf16[1,4096,2,128]{3,2,1,0:T(2,128)(2,1)} copy(bf16[1,4096,2,128]{1,3,2,0:T(8,128)(2,1)} %bitcast.46) | data formatting | bytes 4194304
  266.6 7.3 %convolution_convert_fusion.1 = bf16[256,4096]{1,0:T(8,128)(2,1)} fusion(bf16[1024,4096]{1,0:T(8,128)(2,1)} %all-gather.3.cloned.1.call-done, bf16[1024,512]{1,0:T(8,128)(2,1)} %bitcast.51), kind=kOutput, calls=%fused_computation.7 | convolution fusion | flops 2148532224 | bytes 11010048 | tf_op jit(solution)/shard_map/dot_general | solution.py:382
  273.8 6.2 %copy.15 = bf16[1,4096,2,128]{3,2,1,0:T(2,128)(2,1)} copy(bf16[1,4096,2,128]{1,3,2,0:T(8,128)(2,1)} %bitcast.45) | data formatting | bytes 4194304
  280.0 7.1 %convolution_convert_fusion = bf16[256,4096]{1,0:T(8,128)(2,1)} fusion(bf16[1024,256]{1,0:T(8,128)(2,1)S(1)} %bitcast.48, bf16[1024,4096]{1,0:T(8,128)(2,1)} %all-gather.5.cloned.1.call-done), kind=kOutput, calls=%fused_computation.6 | convolution fusion | flops 2148532224 | bytes 11010048 | tf_op jit(solution)/shard_map/dot_general | solution.py:382
  287.1 52.2 %reduce-scatter.5.cloned.1.call-done = f32[64,4096]{1,0:T(8,128)} async-done(((f32[1024,4096]{1,0:T(8,128)}), f32[64,4096]{1,0:T(8,128)}) %reduce-scatter.5.cloned.1.call-update) | async-done | bytes 1048592 | tf_op jit(solution)/shard_map/reduce_scatter | solution.py:379
  339.2 2.1 convert_element_type.44
  341.3 111.3 %reduce-scatter.3.cloned.1.call-done = f32[64,4096]{1,0:T(8,128)} async-done(((f32[1024,4096]{1,0:T(8,128)}), f32[64,4096]{1,0:T(8,128)}) %reduce-scatter.3.cloned.1.call-update) | async-done | bytes 1048592 | tf_op jit(solution)/shard_map/reduce_scatter | solution.py:357
  452.7 2.1 convert_element_type.42
  (20 shorter events, 3.6 us)
Async XLA Ops:
  7.2 148.7 %copy-start = (bf16[2,128,4096]{2,1,0:T(8,128)(2,1)S(1)}, bf16[2,128,4096]{2,1,0:T(8,128)(2,1)}, u32[]{:S(2)}) copy-start(bf16[2,128,4096]{2,1,0:T(8,128)(2,1)} %param.10) | copy-start | bytes 6291460
  7.2 76.2 %all-gather.3.cloned.1.call-start = ((), (), s32[]{:S(2)}) async-start(), calls=%async_computation.2 | async-start | bytes 8912896 | tf_op jit(solution)/shard_map/all_gather | solution.py:336
  7.9 148.0 %all-gather.5.cloned.1.call-start = ((), (), s32[]{:S(2)}) async-start(), calls=%async_computation.4 | async-start | bytes 8912896 | tf_op jit(solution)/shard_map/all_gather | solution.py:337
  8.7 330.6 %reduce-scatter.5.cloned.1.call-start = ((), (), s32[]{:S(2)}) async-start(), calls=%async_computation.5 | async-start | bytes 17825792 | tf_op jit(solution)/shard_map/reduce_scatter | solution.py:379
  8.7 3.4 copy-start.3
  8.7 3.3 copy-start.4
  164.9 52.5 %copy-start.2 = (bf16[512,8,2,128]{3,1,2,0:T(8,128)(2,1)S(1)}, bf16[512,8,2,128]{3,1,2,0:T(8,128)(2,1)}, u32[]{:S(2)}) copy-start(bf16[512,8,2,128]{3,1,2,0:T(8,128)(2,1)} %copy.23) | copy-start | bytes 6291460
  229.6 1.0 copy-start.1
  229.6 223.1 %reduce-scatter.3.cloned.1.call-start = ((), (), s32[]{:S(2)}) async-start(), calls=%async_computation.3 | async-start | bytes 17825792 | tf_op jit(solution)/shard_map/reduce_scatter | solution.py:357
  238.7 1.0 copy-start.5
Sparse Core Ops, SparseCore 0:
  10.1 73.2 all-gather.2
  85.6 70.2 all-gather.4
  229.7 109.4 reduce-scatter.4
  342.5 110.1 reduce-scatter.2
where the time goes:
time: 467 us; the launch traced here: 461 us
  waiting for transfers between devices  237 us (51%)
  Pallas kernels  106 us (23%)
  matrix products  71.8 us (15%)
  local copies, waits for them, and re-layouts  28.3 us (6%)
  between operations  14 us (3%)
    reduce_scatter x1, waiting for transfers between devices, device_fn(): lax.psum_scatter(y_part, 'tp', scatter_dimension=0, tiled=True).astype(BF16)  111 us
    all_gather x1, waiting for transfers between devices, device_fn(): x_rows = lax.all_gather(x_blk, 'tp', axis=0, tiled=True)  68.5 us
    pallas_call x1, Pallas kernels, device_fn(): attention_call(functools.partial(backward_kernel, n_sh, heads, dim), 'att...  52.5 us
    reduce_scatter x1, waiting for transfers between devices, device_fn(): lax.psum_scatter(dx_part, 'tp', scatter_dimension=0, tiled=True)  52.2 us
    pallas_call x1, Pallas kernels, device_fn(): attention_call(functools.partial(forward_kernel, n_sh, heads, dim), 'attn...  50.7 us
    dot_general x4, matrix products, weight_grad(): lax.dot_general(lhs, rhs, ROWS_CONTRACT, preferred_element_type=F32)  28.7 us
    dot_general x3, matrix products, dot_n(): return jnp.dot(lhs, rhs, preferred_element_type=F32)  24.4 us
    unnamed x16, local copies, waits for them, and re-layouts  24 us
  transfers between devices with their start and end apart: 4, of which 4 were waited for; matrix products, arithmetic and copies ran while one was open for 18% of the time, Pallas kernels for 11%

commit v1 on v0

--- a/solution.py
+++ b/solution.py
@@ -28,6 +28,9 @@
     return jnp.dot(lhs, rhs, preferred_element_type=F32)
 
 
+LINE = 4
+
+
 def block_slot(pos_blk, n_sh):
     return jnp.where(pos_blk < n_sh, 2 * pos_blk, 2 * (2 * n_sh - 1 - pos_blk) + 1)
 
@@ -79,13 +82,62 @@
             for copy in copies(name):
                 copy.wait_send()
 
-    def barrier():
+    def barrier(others=()):
         sem = pltpu.get_barrier_semaphore()
-        for target in ((1, 0), (n_x - 1, 0), (0, 1)):
-            pl.semaphore_signal(sem, inc=1, device_id={"cp": rank_of(*target)}, device_id_type=pl.DeviceIdType.MESH)
-        pl.semaphore_wait(sem, 3)
+        for target in [{"cp": rank_of(*offset)} for offset in ((1, 0), (n_x - 1, 0), (0, 1))] + list(others):
+            pl.semaphore_signal(sem, inc=1, device_id=target, device_id_type=pl.DeviceIdType.MESH)
+        pl.semaphore_wait(sem, 3 + len(others))
 
     return rank, rank_of, barrier, start, wait_recv, wait_sends
+
+
+def line_device(shift):
+    tp_idx = lax.axis_index("tp")
+    return {"tp": LINE * (tp_idx // LINE) + lax.rem(lax.rem(tp_idx, LINE) + shift + LINE, LINE)}
+
+
+def weight_gather(w_ref, all_ref, other_core, sends, recvs):
+    core = lax.rem(lax.axis_index("cp"), 2)
+    part_rows = w_ref.shape[0] // 2
+    quarter = part_rows // 2
+    first = core * part_rows
+
+    def whole(slot):
+        return all_ref.at[slot, pl.ds(first, part_rows)]
+
+    def lo(slot):
+        return all_ref.at[slot, pl.ds(first, quarter)]
+
+    def hi(slot):
+        return all_ref.at[slot, pl.ds(first + quarter, quarter)]
+
+    own = w_ref.at[pl.ds(first, part_rows)]
+    routes = [
+        ("prev", own, whole(1), line_device(1)), ("next", own, whole(2), line_device(-1)),
+        ("far_lo", lo(1), lo(3), line_device(1)), ("far_hi", hi(2), hi(3), line_device(-1)),
+        ("prev_x", whole(1), whole(1), other_core), ("next_x", whole(2), whole(2), other_core),
+        ("far_lo_x", lo(3), lo(3), other_core), ("far_hi_x", hi(3), hi(3), other_core),
+    ]
+
+    def copy_of(name):
+        for idx, (kind, src, dst, target) in enumerate(routes):
+            if kind == name:
+                return pltpu.make_async_remote_copy(src_ref=src, dst_ref=dst, send_sem=sends.at[idx], recv_sem=recvs.at[idx],
+                                                    device_id=target, device_id_type=pl.DeviceIdType.MESH)
+
+    def start(*names):
+        for name in names:
+            copy_of(name).start()
+
+    def wait_recv(*names):
+        for name in names:
+            copy_of(name).wait_recv()
+
+    def wait_sends():
+        for route in routes:
+            copy_of(route[0]).wait_send()
+
+    return start, wait_recv, wait_sends
 
 
 def causal_mask(rows, cols, transposed=False):
@@ -94,14 +146,19 @@
     return col_ids >= row_ids if transposed else row_ids >= col_ids
 
 
-def forward_kernel(n_sh, heads, dim, q_ref, kv_ref, o_ref, lse_ref, all_ref, kv_buf, m_ref, l_ref, acc_ref, sends, recvs, sems):
+def forward_kernel(n_sh, heads, dim, q_ref, kv_ref, wo_ref, o_ref, lse_ref, all_ref, wo_all_ref,
+                   kv_buf, m_ref, l_ref, acc_ref, sends, recvs, w_sends, w_recvs, sems):
     rank, rank_of, barrier, start, wait_recv, wait_sends = shard_exchange(n_sh, [(kv_ref, kv_buf)], sends, recvs)
     n_x = n_sh // 2
-    barrier()
+    w_start, w_wait, w_wait_sends = weight_gather(wo_ref, wo_all_ref, {"cp": rank_of(0, 1)}, w_sends, w_recvs)
+    barrier([line_device(1), line_device(-1)])
     start("prev", "next", "own_x")
+    w_start("prev", "next")
     width = heads * dim
     half_rows = q_ref.shape[1]
     log2e_scale = math.log2(math.e) * dim ** -0.5
+    own_w = pltpu.make_async_copy(wo_ref, wo_all_ref.at[0], sems.at[1])
+    own_w.start()
     own = pltpu.make_async_copy(kv_ref, kv_buf.at[pl.ds(2 * rank, 2)], sems.at[0])
     own.start()
     own.wait()
@@ -161,6 +218,10 @@
     wait_recv("next")
     start("far_hi", "next_x")
     visit(4, 4, shard_of)
+    w_wait("prev")
+    w_start("far_lo", "prev_x")
+    w_wait("next")
+    w_start("far_hi", "next_x")
     wait_recv("prev_x", "next_x")
     visit(8, 2, shard_of)
     wait_recv("far_lo", "far_hi")
@@ -170,6 +231,8 @@
     out = pltpu.make_async_copy(kv_buf, all_ref, sems.at[0])
     out.start()
     visit(14, 2, shard_of)
+    w_wait("far_lo", "far_hi")
+    w_start("far_lo_x", "far_hi_x")
     for half in range(2):
         for h in range(heads):
             cols = slice(h * dim, (h + 1) * dim)
@@ -178,20 +241,44 @@
             lse = m_ref[half, h] * log2e_scale + jnp.log2(l)
             lse_ref[half, h:h + 1, :] = jnp.transpose(lse)[:1]
     out.wait()
+    own_w.wait()
+    w_wait("prev_x", "next_x", "far_lo_x", "far_hi_x")
     wait_sends()
-
-
-def stats_kernel(heads, dim, o_ref, do_ref, lse_ref, out_ref):
-    half_rows = o_ref.shape[1]
+    w_wait_sends()
+
+
+def stats_kernel(heads, dim, o_ref, do_ref, lse_ref, out_ref, rows_ref, o_buf, sends, recvs):
+    y_pos = lax.rem(lax.axis_index("tp"), LINE)
+    shifts = (0, 1, -1, 2)
+    sem = pltpu.get_barrier_semaphore()
+    for shift in shifts[1:]:
+        pl.semaphore_signal(sem, inc=1, device_id=line_device(shift), device_id_type=pl.DeviceIdType.MESH)
+    pl.semaphore_wait(sem, 3)
+    copies = []
+    for slot in range(1, LINE):
+        target = line_device(shifts[slot])
+        copies.append(pltpu.make_async_remote_copy(
+            src_ref=o_ref.at[:, lax.rem(target["tp"], LINE)], dst_ref=o_buf.at[slot - 1], send_sem=sends.at[slot - 1],
+            recv_sem=recvs.at[slot - 1], device_id=target, device_id_type=pl.DeviceIdType.MESH))
+        copies[-1].start()
+    width = heads * dim
+    rows_ref[:, :, :width] = o_ref[:, y_pos]
+    half_rows = lse_ref.shape[2]
+    o_rows = o_ref[...].reshape(2, half_rows, width)
     for half in range(2):
         rows = [lse_ref[half]]
         for h in range(heads):
             cols = slice(h * dim, (h + 1) * dim)
-            prod = do_ref[half, :, cols].astype(F32) * o_ref[half, :, cols].astype(F32)
+            prod = do_ref[half, :, cols].astype(F32) * o_rows[half, :, cols].astype(F32)
             delta = jnp.broadcast_to(jnp.sum(prod, axis=1, keepdims=True), (half_rows, dim))
             rows.append(jnp.transpose(delta)[:1])
         rows.append(jnp.zeros((8 - 2 * heads, half_rows), F32))
         out_ref[half] = jnp.concatenate(rows, axis=0)
+    for slot in range(1, LINE):
+        copies[slot - 1].wait_recv()
+        rows_ref[:, :, slot * width:(slot + 1) * width] = o_buf[slot - 1]
+    for copy in copies:
+        copy.wait_send()
 
 
 def backward_kernel(n_sh, heads, dim, q_ref, do_ref, st_ref, all_ref, dq_ref, dkv_ref,
@@ -345,23 +432,30 @@
         dma = pltpu.SemaphoreType.DMA
         kv_all_shape = (2 * n_sh, half_rows, 2 * width)
 
-        o, lse, kv_all = attention_call(
+        o, lse, kv_all, wo_all = attention_call(
             functools.partial(forward_kernel, n_sh, heads, dim), "attn_fwd", 0, 2 * tile_flops,
-            [VMEM_SPEC, VMEM_SPEC], [VMEM_SPEC, VMEM_SPEC, ANY_SPEC],
+            [VMEM_SPEC] * 3, [VMEM_SPEC, VMEM_SPEC, ANY_SPEC, ANY_SPEC],
             [jax.ShapeDtypeStruct((2, half_rows, width), BF16), jax.ShapeDtypeStruct((2, heads, half_rows), F32),
-             jax.ShapeDtypeStruct(kv_all_shape, BF16)],
-            [pltpu.VMEM(kv_all_shape, BF16), acc, acc, acc, dma((9,)), dma((9,)), dma((1,))],
-        )(q, kv)
+             jax.ShapeDtypeStruct(kv_all_shape, BF16), jax.ShapeDtypeStruct((LINE, width, model_dim), BF16)],
+            [pltpu.VMEM(kv_all_shape, BF16), acc, acc, acc, dma((9,)), dma((9,)), dma((8,)), dma((8,)), dma((2,))],
+        )(q, kv, wo)
         o_flat = o.reshape(n_rows, width)
-        y_part = dot_n(o_flat, wo)
-        y_blk = lax.psum_scatter(y_part, "tp", scatter_dimension=0, tiled=True).astype(BF16)
-
         d_o = dot_t(dy_rows, wo).astype(BF16).reshape(2, half_rows, width)
-        stats = pl.pallas_call(
+        n_z = mesh.shape["tp"] // LINE
+        blk_rows = n_rows // mesh.shape["tp"]
+        stats, o_rows = pl.pallas_call(
             functools.partial(stats_kernel, heads, dim),
             name="attn_stats",
-            out_shape=jax.ShapeDtypeStruct((2, 8, half_rows), F32),
-        )(o, d_o, lse)
+            out_shape=[jax.ShapeDtypeStruct((2, 8, half_rows), F32), jax.ShapeDtypeStruct((n_z, blk_rows, LINE * width), BF16)],
+            in_specs=[VMEM_SPEC] * 3,
+            out_specs=[VMEM_SPEC] * 2,
+            scratch_shapes=[pltpu.VMEM((LINE - 1, n_z, blk_rows, width), BF16), dma((LINE - 1,)), dma((LINE - 1,))],
+            compiler_params=pltpu.CompilerParams(collective_id=2, has_side_effects=True),
+        )(o.reshape(n_z, LINE, blk_rows, width), d_o, lse)
+        y_part = dot_n(o_rows.reshape(n_z * blk_rows, LINE * width), wo_all.reshape(LINE * width, model_dim))
+        y_part, stats = lax.optimization_barrier((y_part, stats))
+        columns = [[LINE * z_idx + y_idx for z_idx in range(n_z)] for y_idx in range(LINE)]
+        y_blk = lax.psum_scatter(y_part, "tp", scatter_dimension=0, axis_index_groups=columns, tiled=True).astype(BF16)
         shard_buf = pltpu.VMEM((2 * n_sh, half_rows, width), BF16)
         dq, dkv = attention_call(
             functools.partial(backward_kernel, n_sh, heads, dim), "attn_bwd", 1, 7 * tile_flops // 2,

time: 467 us -> 391 us (0.84)
  waiting for transfers between devices: 237 us -> 150 us
  Pallas kernels: 106 us -> 132 us
  local copies, waits for them, and re-layouts: 28.3 us -> 19 us
    reduce_scatter x1, waiting for transfers between devices: 111 us -> 0.01 us  [device_fn(): lax.psum_scatter(y_part, 'tp', scatter_dimension=0, axis_index_groups=col...]
    reduce_scatter x1, waiting for transfers between devices: 52.2 us -> 69.8 us  [device_fn(): lax.psum_scatter(dx_part, 'tp', scatter_dimension=0, tiled=True)]
    pallas_call x1, Pallas kernels: 50.7 us -> 67.5 us  [device_fn(): attention_call(functools.partial(forward_kernel, n_sh, heads, dim), 'attn...]
    unnamed x16 -> x14, local copies, waits for them, and re-layouts: 24 us -> 12.6 us
    pallas_call x1, Pallas kernels: 2.42 us -> 12 us  [device_fn(): pl.pallas_call(functools.partial(stats_kernel, heads, dim), name='attn_st...]
    all_gather x1, waiting for transfers between devices: 4.02 us -> 8.94 us  [device_fn(): dy_rows = lax.all_gather(dy_blk, 'tp', axis=0, tiled=True)]
  transfers between devices with their start and end apart: 4 -> 4, of which waited for: 4 -> 3; matrix products, arithmetic and copies ran while one was open for 18% -> 19% of each run, Pallas kernels for 11% -> 31%
where the time goes in v1:
time: 391 us; the launch traced here: 386 us
  waiting for transfers between devices  150 us (38%)
  Pallas kernels  132 us (34%)
  matrix products  67.3 us (17%)
  local copies, waits for them, and re-layouts  19 us (5%)
  between operations  14 us (4%)
  other arithmetic  4.14 us (1%)
    all_gather x1, waiting for transfers between devices, device_fn(): x_rows = lax.all_gather(x_blk, 'tp', axis=0, tiled=True)  69.8 us
    reduce_scatter x1, waiting for transfers between devices, device_fn(): lax.psum_scatter(dx_part, 'tp', scatter_dimension=0, tiled=True)  69.8 us
    pallas_call x1, Pallas kernels, device_fn(): attention_call(functools.partial(forward_kernel, n_sh, heads, dim), 'attn...  67.5 us
    pallas_call x1, Pallas kernels, device_fn(): attention_call(functools.partial(backward_kernel, n_sh, heads, dim), 'att...  52 us
    dot_general x4, matrix products, weight_grad(): lax.dot_general(lhs, rhs, ROWS_CONTRACT, preferred_element_type=F32)  24.4 us
    dot_general x3, matrix products, dot_n(): return jnp.dot(lhs, rhs, preferred_element_type=F32)  23.8 us
    dot_general x2, matrix products, dot_t(): return lax.dot_general(lhs, rhs, COLS_CONTRACT, preferred_element_type=F32)  19.2 us
    unnamed x14, local copies, waits for them, and re-layouts  12.6 us
  transfers between devices with their start and end apart: 4, of which 3 were waited for; matrix products, arithmetic and copies ran while one was open for 19% of the time, Pallas kernels for 31%

profile of v1, /device:TPU:0, one launch (start us, length us, event | category | flops | bytes accessed | tf_op | source)
XLA Modules:
  0.0 386.1 jit_solution(6018571918648871428)
XLA Ops:
  7.9 0.7 all-gather.5.cloned.1.call-update
  8.7 4.9 %copy_bitcast_fusion = (bf16[4096,256]{1,0:T(8,128)(2,1)}, bf16[4096,256]{1,0:T(8,128)(2,1)}) fusion(bf16[512,8,2,128]{3,2,1,0:T(2,128)(2,1)} %bitcast.57, bf16[512,8,2,128]{3,2,1,0:T(2,128)(2,1)} %bitcast.58), kind=kLoop, calls=%fused_computation.14 | loop fusion | bytes 8388608 | tf_op jit(solution)/shard_map/reshape | solution.py:420
  13.6 69.8 %all-gather.3.cloned.1.call-done = bf16[1024,4096]{1,0:T(8,128)(2,1)} async-done(((bf16[64,4096]{1,0:T(8,128)(2,1)}), bf16[1024,4096]{1,0:T(8,128)(2,1)}) %all-gather.3.cloned.1.call-update) | async-done | bytes 8388624 | tf_op jit(solution)/shard_map/all_gather | solution.py:423
  83.4 9.3 %fusion.16 = bf16[1024,512]{0,1:T(8,128)(2,1)S(1)} fusion(bf16[1024,4096]{1,0:T(8,128)(2,1)} %all-gather.3.cloned.1.call-done, bf16[4096,256]{1,0:T(8,128)(2,1)} %get-tuple-element.32, bf16[4096,256]{1,0:T(8,128)(2,1)} %get-tuple-element.33), kind=kOutput, calls=%fused_computation.21 | convolution fusion | flops 4303880192 | bytes 13631488 | tf_op jit(solution)/shard_map/dot_general | solution.py:28
  92.7 1.5 copy.12
  94.2 6.5 %convolution_convert_fusion.5 = bf16[1024,256]{1,0:T(8,128)(2,1)} fusion(bf16[1024,4096]{1,0:T(8,128)(2,1)} %all-gather.3.cloned.1.call-done, bf16[512,8,2,128]{3,2,1,0:T(2,128)(2,1)S(1)} %bitcast.54), kind=kOutput, calls=%fused_computation.23 | convolution fusion | flops 2147745792 | bytes 11010048 | tf_op jit(solution)/shard_map/dot_general | solution.py:28
  100.8 67.5 %attn_fwd.1 = (bf16[2,512,256]{2,1,0:T(8,128)(2,1)}, f32[2,2,512]{2,1,0:T(2,128)}, bf16[16,512,512]{2,1,0:T(8,128)(2,1)}, bf16[4,256,4096]{2,1,0:T(8,128)(2,1)}) custom-call(bf16[2,512,256]{2,1,0:T(8,128)(2,1)} %bitcast.68, bf16[2,512,512]{2,1,0:T(8,128)(2,1)} %bitcast.59, bf16[256,4096]{1,0:T(8,128)(2,1)} %bitcast.64), custom_call_target="tpu_custom_call" | custom-call | flops 9126805504 | bytes 10485760 | tf_op jit(solution)/shard_map/attn_fwd/pallas_call | solution.py:435
  168.3 8.9 %all-gather.5.cloned.1.call-done = bf16[1024,4096]{1,0:T(8,128)(2,1)} async-done(((bf16[64,4096]{1,0:T(8,128)(2,1)}), bf16[1024,4096]{1,0:T(8,128)(2,1)}) %all-gather.5.cloned.1.call-update) | async-done | bytes 8388624 | tf_op jit(solution)/shard_map/all_gather | solution.py:424
  177.2 7.1 %convolution_convert_fusion.4 = bf16[1024,256]{1,0:T(8,128)(2,1)} fusion(bf16[1024,4096]{1,0:T(8,128)(2,1)} %all-gather.5.cloned.1.call-done, bf16[256,4096]{1,0:T(8,128)(2,1)} %bitcast.65), kind=kOutput, calls=%fused_computation.22 | convolution fusion | flops 2147745792 | bytes 11010048 | tf_op jit(solution)/shard_map/dot_general | solution.py:24
  184.4 12.0 %attn_stats.1 = (f32[2,8,512]{2,1,0:T(8,128)}, bf16[4,64,1024]{2,1,0:T(8,128)(2,1)}) custom-call(bf16[4,4,64,256]{3,2,1,0:T(8,128)(2,1)} %bitcast.48, bf16[2,512,256]{2,1,0:T(8,128)(2,1)} %bitcast.62, f32[2,2,512]{2,1,0:T(2,128)} %get-tuple-element.17.lse_ref), custom_call_target="tpu_custom_call" | custom-call | tf_op jit(solution)/shard_map/attn_stats/pallas_call | solution.py:446
  196.3 8.0 %fusion.23 = f32[256,4096]{1,0:T(8,128)} fusion(bf16[256,1024]{1,0:T(8,128)(2,1)} %bitcast.66, bf16[1024,4096]{1,0:T(8,128)(2,1)} %bitcast.67), kind=kOutput, calls=%fused_computation.28 | convolution fusion | flops 2147483648 | bytes 13107200 | tf_op jit(solution)/shard_map/dot_general | solution.py:28
  204.7 52.0 %attn_bwd.1 = (bf16[2,512,256]{2,1,0:T(8,128)(2,1)}, bf16[2,512,512]{2,1,0:T(8,128)(2,1)}) custom-call(bf16[2,512,256]{2,1,0:T(8,128)(2,1)} %bitcast.69, bf16[2,512,256]{2,1,0:T(8,128)(2,1)} %bitcast.63, f32[2,8,512]{2,1,0:T(8,128)} %get-tuple-element.22.st_ref, bf16[16,512,512]{2,1,0:T(8,128)(2,1)} %get-tuple-element.23.all_ref), custom_call_target="tpu_custom_call" | custom-call | flops 15971909632 | bytes 10485760 | tf_op jit(solution)/shard_map/attn_bwd/pallas_call | solution.py:460
  256.7 12.0 %fusion = f32[1024,4096]{1,0:T(8,128)} fusion(bf16[4096,256]{1,0:T(8,128)(2,1)S(1)} %copy-done.3, bf16[4096,256]{1,0:T(8,128)(2,1)} %get-tuple-element.33, bf16[4096,256]{1,0:T(8,128)(2,1)S(1)} %bitcast.56, bf16[1024,512]{1,0:T(8,128)(2,1)} %bitcast.50, bf16[1024,256]{1,0:T(8,128)(2,1)} %bitcast.60), kind=kOutput, calls=%fused_computation | convolution fusion | flops 6464471040 | bytes 24641536 | tf_op jit(solution)/shard_map/dot_general | solution.py:24
  268.8 1.0 copy-done.4
  269.8 5.8 %convolution_convert_fusion.3 = bf16[256,4096]{1,0:T(8,128)(2,1)S(1)} fusion(bf16[1024,256]{1,0:T(8,128)(2,1)S(1)} %bitcast.61, bf16[1024,4096]{1,0:T(8,128)(2,1)} %all-gather.3.cloned.1.call-done), kind=kOutput, calls=%fused_computation.9 | convolution fusion | flops 2148532224 | bytes 11010048 | tf_op jit(solution)/shard_map/dot_general | solution.py:476
  275.5 3.8 copy.13
  279.3 5.8 %convolution_convert_fusion.2 = bf16[256,4096]{1,0:T(8,128)(2,1)S(1)} fusion(bf16[1024,4096]{1,0:T(8,128)(2,1)} %all-gather.3.cloned.1.call-done, bf16[1024,512]{1,0:T(8,128)(2,1)S(1)} %bitcast.51), kind=kOutput, calls=%fused_computation.8 | convolution fusion | flops 2148532224 | bytes 11010048 | tf_op jit(solution)/shard_map/dot_general | solution.py:476
  285.1 3.8 copy.14
  288.9 5.8 %convolution_convert_fusion.1 = bf16[256,4096]{1,0:T(8,128)(2,1)S(1)} fusion(bf16[1024,4096]{1,0:T(8,128)(2,1)} %all-gather.3.cloned.1.call-done, bf16[1024,512]{1,0:T(8,128)(2,1)S(1)} %bitcast.52), kind=kOutput, calls=%fused_computation.7 | convolution fusion | flops 2148532224 | bytes 11010048 | tf_op jit(solution)/shard_map/dot_general | solution.py:476
  294.6 3.8 copy.15
  298.4 7.1 %convolution_convert_fusion = bf16[256,4096]{1,0:T(8,128)(2,1)} fusion(bf16[1024,256]{1,0:T(8,128)(2,1)S(1)} %bitcast.49, bf16[1024,4096]{1,0:T(8,128)(2,1)} %all-gather.5.cloned.1.call-done), kind=kOutput, calls=%fused_computation.6 | convolution fusion | flops 2148532224 | bytes 11010048 | tf_op jit(solution)/shard_map/dot_general | solution.py:476
  305.5 2.1 convert_element_type.43
  307.6 69.8 %reduce-scatter.5.cloned.1.call-done = f32[64,4096]{1,0:T(8,128)} async-done(((f32[1024,4096]{1,0:T(8,128)}), f32[64,4096]{1,0:T(8,128)}) %reduce-scatter.5.cloned.1.call-update) | async-done | bytes 1048592 | tf_op jit(solution)/shard_map/reduce_scatter | solution.py:473
  377.3 2.1 convert_element_type.44
  (18 shorter events, 1.2 us)
Async XLA Ops:
  7.2 76.2 %all-gather.3.cloned.1.call-start = ((), (), s32[]{:S(2)}) async-start(), calls=%async_computation.2 | async-start | bytes 8912896 | tf_op jit(solution)/shard_map/all_gather | solution.py:423
  7.9 169.3 %all-gather.5.cloned.1.call-start = ((), (), s32[]{:S(2)}) async-start(), calls=%async_computation.3 | async-start | bytes 8912896 | tf_op jit(solution)/shard_map/all_gather | solution.py:424
  8.6 296.8 %reduce-scatter.3.cloned.1.call-start = ((), (), s32[]{:S(2)}) async-start(), calls=%async_computation.4 | async-start | bytes 5242880 | tf_op jit(solution)/shard_map/reduce_scatter | solution.py:458
  83.4 10.8 %copy-start.2 = (bf16[4096,2,128]{2,1,0:T(2,128)(2,1)S(1)}, bf16[4096,2,128]{2,1,0:T(2,128)(2,1)}, u32[]{:S(2)}) copy-start(bf16[4096,2,128]{2,1,0:T(2,128)(2,1)} %param.7) | copy-start | bytes 6291460
  204.3 173.0 %reduce-scatter.5.cloned.1.call-start = ((), (), s32[]{:S(2)}) async-start(), calls=%async_computation.5 | async-start | bytes 17825792 | tf_op jit(solution)/shard_map/reduce_scatter | solution.py:473
  204.7 52.0 %copy-start.3 = (bf16[4096,256]{1,0:T(8,128)(2,1)S(1)}, bf16[4096,256]{1,0:T(8,128)(2,1)}, u32[]{:S(2)}) copy-start(bf16[4096,256]{1,0:T(8,128)(2,1)} %get-tuple-element.32) | copy-start | bytes 6291460
  268.7 1.0 copy-start.4
  275.5 3.8 copy-start.1
  294.6 3.8 copy-start
Sparse Core Ops, SparseCore 0:
  10.1 73.2 all-gather.2
  85.5 91.6 all-gather.4
  204.5 46.0 reduce-scatter.2
  268.9 108.4 reduce-scatter.4

commit v2 on v1

--- a/solution.py
+++ b/solution.py
@@ -96,20 +96,20 @@
     return {"tp": LINE * (tp_idx // LINE) + lax.rem(lax.rem(tp_idx, LINE) + shift + LINE, LINE)}
 
 
-def weight_gather(w_ref, all_ref, other_core, sends, recvs):
+def weight_gather(w_ref, slot_ref, other_core, sends, recvs):
     core = lax.rem(lax.axis_index("cp"), 2)
     part_rows = w_ref.shape[0] // 2
     quarter = part_rows // 2
     first = core * part_rows
 
     def whole(slot):
-        return all_ref.at[slot, pl.ds(first, part_rows)]
+        return slot_ref(slot).at[pl.ds(first, part_rows)]
 
     def lo(slot):
-        return all_ref.at[slot, pl.ds(first, quarter)]
+        return slot_ref(slot).at[pl.ds(first, quarter)]
 
     def hi(slot):
-        return all_ref.at[slot, pl.ds(first + quarter, quarter)]
+        return slot_ref(slot).at[pl.ds(first + quarter, quarter)]
 
     own = w_ref.at[pl.ds(first, part_rows)]
     routes = [
@@ -150,7 +150,7 @@
                    kv_buf, m_ref, l_ref, acc_ref, sends, recvs, w_sends, w_recvs, sems):
     rank, rank_of, barrier, start, wait_recv, wait_sends = shard_exchange(n_sh, [(kv_ref, kv_buf)], sends, recvs)
     n_x = n_sh // 2
-    w_start, w_wait, w_wait_sends = weight_gather(wo_ref, wo_all_ref, {"cp": rank_of(0, 1)}, w_sends, w_recvs)
+    w_start, w_wait, w_wait_sends = weight_gather(wo_ref, lambda slot: wo_all_ref.at[slot], {"cp": rank_of(0, 1)}, w_sends, w_recvs)
     barrier([line_device(1), line_device(-1)])
     start("prev", "next", "own_x")
     w_start("prev", "next")
@@ -281,13 +281,16 @@
         copy.wait_send()
 
 
-def backward_kernel(n_sh, heads, dim, q_ref, do_ref, st_ref, all_ref, dq_ref, dkv_ref,
-                    kv_buf, q_buf, do_buf, st_buf, acc_ref, lse_ref, dot_ref, dk_acc, dv_acc, sends, recvs, sems):
+def backward_kernel(n_sh, heads, dim, q_ref, do_ref, st_ref, all_ref, w_ref, dq_ref, dkv_ref, w_prev_ref, w_next_ref, w_far_ref,
+                    kv_buf, q_buf, do_buf, st_buf, acc_ref, lse_ref, dot_ref, dk_acc, dv_acc, sends, recvs, w_sends, w_recvs, sems):
     rank, rank_of, barrier, start, wait_recv, wait_sends = shard_exchange(
         n_sh, [(q_ref, q_buf), (do_ref, do_buf), (st_ref, st_buf)], sends, recvs)
     n_x = n_sh // 2
-    barrier()
+    w_slots = (None, w_prev_ref, w_next_ref, w_far_ref)
+    w_start, w_wait, w_wait_sends = weight_gather(w_ref, lambda slot: w_slots[slot], {"cp": rank_of(0, 1)}, w_sends, w_recvs)
+    barrier([line_device(1), line_device(-1)])
     start("prev", "next", "own_x")
+    w_start("prev", "next")
     load = [pltpu.make_async_copy(all_ref, kv_buf, sems.at[0])]
     for idx, (own, buf) in enumerate([(q_ref, q_buf), (do_ref, do_buf), (st_ref, st_buf)]):
         load.append(pltpu.make_async_copy(own, buf.at[pl.ds(2 * rank, 2)], sems.at[1 + idx]))
@@ -376,7 +379,12 @@
 
     visit(0, 1)
     wait_recv("own_x")
-    visit(2, 6)
+    visit(2, 2)
+    w_wait("prev")
+    w_start("far_lo", "prev_x")
+    w_wait("next")
+    w_start("far_hi", "next_x")
+    visit(4, 4)
     wait_recv("prev_x", "next_x")
     visit(8, 2)
     wait_recv("far_lo", "far_hi")
@@ -384,13 +392,138 @@
     visit(10, 4)
     wait_recv("far_lo_x", "far_hi_x")
     visit(14, 2)
+    w_wait("far_lo", "far_hi")
+    w_start("far_lo_x", "far_hi_x")
     for half in range(2):
         for h in range(heads):
             cols = slice(h * dim, (h + 1) * dim)
             vcols = slice(width + h * dim, width + (h + 1) * dim)
             dkv_ref[half, :, cols] = (dk_acc[half, h] * scale).astype(BF16)
             dkv_ref[half, :, vcols] = dv_acc[half, h].astype(BF16)
+    w_wait("prev_x", "next_x", "far_lo_x", "far_hi_x")
     wait_sends()
+    w_wait_sends()
+
+
+def grad_rows_kernel(dq_ref, dkv_ref, own_ref, prev_ref, next_ref, far_ref, dq_buf, dkv_buf, sends, recvs):
+    y_pos = lax.rem(lax.axis_index("tp"), LINE)
+    shifts = (0, 1, -1, 2)
+    sem = pltpu.get_barrier_semaphore()
+    for shift in shifts[1:]:
+        pl.semaphore_signal(sem, inc=1, device_id=line_device(shift), device_id_type=pl.DeviceIdType.MESH)
+    pl.semaphore_wait(sem, LINE - 1)
+    copies = []
+    for slot in range(1, LINE):
+        target = line_device(shifts[slot])
+        for idx, (src, buf) in enumerate([(dq_ref, dq_buf), (dkv_ref, dkv_buf)]):
+            copies.append(pltpu.make_async_remote_copy(
+                src_ref=src.at[:, lax.rem(target["tp"], LINE)], dst_ref=buf.at[slot - 1], send_sem=sends.at[2 * slot - 2 + idx],
+                recv_sem=recvs.at[2 * slot - 2 + idx], device_id=target, device_id_type=pl.DeviceIdType.MESH))
+            copies[-1].start()
+    width = dq_ref.shape[3]
+    own_ref[:, :, :width] = dq_ref[:, y_pos]
+    own_ref[:, :, width:] = dkv_ref[:, y_pos]
+    for copy in copies:
+        copy.wait_recv()
+    for slot, out_ref in enumerate((prev_ref, next_ref, far_ref)):
+        out_ref[:, :, :width] = dq_buf[slot]
+        out_ref[:, :, width:] = dkv_buf[slot]
+    for copy in copies:
+        copy.wait_send()
+
+
+def gather_rows_kernel(x_ref, all_ref, sends, recvs, sem):
+    tp_idx = lax.axis_index("tp")
+    pos = (tp_idx // LINE, lax.rem(tp_idx, LINE))
+    half_rows = x_ref.shape[0] // 2
+    quarter = half_rows // 2
+
+    def block(axis, fast, slow):
+        off = (slow, fast) if axis == 1 else (fast, slow)
+        z_idx, y_idx = [lax.rem(base + shift + LINE, LINE) for base, shift in zip(pos, off)]
+        return LINE * z_idx + y_idx
+
+    barrier = pltpu.get_barrier_semaphore()
+    for axis in range(2):
+        for shift in (1, -1):
+            pl.semaphore_signal(barrier, inc=1, device_id={"tp": block(axis, shift, 0)}, device_id_type=pl.DeviceIdType.MESH)
+    pl.semaphore_wait(barrier, 4)
+
+    own = pltpu.make_async_copy(x_ref, all_ref.at[block(1, 0, 0)], sem.at[0])
+    own.start()
+    table = {}
+    for colour in range(2):
+        axis = 1 - colour
+        base = colour * half_rows
+        whole, low, high = (base, half_rows), (base, quarter), (base + quarter, quarter)
+
+        def add(name, fast, slow, rows, along_fast, shift):
+            idx = len(table)
+            span = pl.ds(*rows)
+            blk = block(axis, fast, slow)
+            src = x_ref.at[span] if fast == 0 and slow == 0 else all_ref.at[blk, span]
+            target = block(axis, shift, 0) if along_fast else block(axis, 0, shift)
+            table[colour, name] = pltpu.make_async_remote_copy(
+                src_ref=src, dst_ref=all_ref.at[blk, span], send_sem=sends.at[idx], recv_sem=recvs.at[idx],
+                device_id={"tp": target}, device_id_type=pl.DeviceIdType.MESH)
+
+        add("prev", 0, 0, whole, True, 1)
+        add("next", 0, 0, whole, True, -1)
+        add("far_lo", -1, 0, low, True, 1)
+        add("far_hi", 1, 0, high, True, -1)
+        for fast in (0, -1, 1, 2):
+            add(("prev", fast), fast, 0, whole, False, 1)
+            add(("next", fast), fast, 0, whole, False, -1)
+            add(("far_lo", fast), fast, -1, low, False, 1)
+            add(("far_hi", fast), fast, 1, high, False, -1)
+
+    def start(*names):
+        for name in names:
+            for colour in range(2):
+                table[colour, name].start()
+
+    def wait(*names):
+        for name in names:
+            for colour in range(2):
+                table[colour, name].wait_recv()
+
+    start("prev", "next", ("prev", 0), ("next", 0))
+    wait("prev")
+    start("far_lo", ("prev", -1), ("next", -1))
+    wait("next")
+    start("far_hi", ("prev", 1), ("next", 1))
+    wait(("prev", 0))
+    start(("far_lo", 0))
+    wait(("next", 0))
+    start(("far_hi", 0))
+    wait("far_lo", "far_hi")
+    start(("prev", 2), ("next", 2))
+    for fast in (-1, 1, 2):
+        wait(("prev", fast))
+        start(("far_lo", fast))
+        wait(("next", fast))
+        start(("far_hi", fast))
+    for fast in (0, -1, 1, 2):
+        wait(("far_lo", fast), ("far_hi", fast))
+    own.wait()
+    for copy in table.values():
+        copy.wait_send()
+
+
+def gather_rows(x_blk, n_tp):
+    rows, cols = x_blk.shape
+    if n_tp != LINE * LINE:
+        return lax.all_gather(x_blk, "tp", axis=0, tiled=True)
+    gathered = pl.pallas_call(
+        gather_rows_kernel,
+        name="gather_rows",
+        out_shape=jax.ShapeDtypeStruct((n_tp, rows, cols), x_blk.dtype),
+        in_specs=[VMEM_SPEC],
+        out_specs=ANY_SPEC,
+        scratch_shapes=[pltpu.SemaphoreType.DMA((40,)), pltpu.SemaphoreType.DMA((40,)), pltpu.SemaphoreType.DMA((1,))],
+        compiler_params=pltpu.CompilerParams(collective_id=4, has_side_effects=True),
+    )(x_blk)
+    return gathered.reshape(n_tp * rows, cols)
 
 
 VMEM_SPEC = pl.BlockSpec(memory_space=pltpu.VMEM)
@@ -420,7 +553,8 @@
         wkv = jnp.concatenate([w_key.reshape(model_dim, width), w_value.reshape(model_dim, width)], axis=1)
         wo = w_out.reshape(width, model_dim)
 
-        x_rows = lax.all_gather(x_blk, "tp", axis=0, tiled=True)
+        x_rows = gather_rows(x_blk, mesh.shape["tp"])
+        x_rows, dy_blk = lax.optimization_barrier((x_rows, dy_blk))
         dy_rows = lax.all_gather(dy_blk, "tp", axis=0, tiled=True)
         n_rows = x_rows.shape[0]
         half_rows = n_rows // 2
@@ -440,6 +574,10 @@
             [pltpu.VMEM(kv_all_shape, BF16), acc, acc, acc, dma((9,)), dma((9,)), dma((8,)), dma((8,)), dma((2,))],
         )(q, kv, wo)
         o_flat = o.reshape(n_rows, width)
+        lse, *late_weights = lax.optimization_barrier((lse, w_query, w_key, w_value))
+        w_all = jnp.concatenate([w_late.reshape(model_dim, width) for w_late in late_weights], axis=1)
+        n_cols = model_dim // 2
+        w_shared = w_all[n_cols:]
         d_o = dot_t(dy_rows, wo).astype(BF16).reshape(2, half_rows, width)
         n_z = mesh.shape["tp"] // LINE
         blk_rows = n_rows // mesh.shape["tp"]
@@ -455,22 +593,39 @@
         y_part = dot_n(o_rows.reshape(n_z * blk_rows, LINE * width), wo_all.reshape(LINE * width, model_dim))
         y_part, stats = lax.optimization_barrier((y_part, stats))
         columns = [[LINE * z_idx + y_idx for z_idx in range(n_z)] for y_idx in range(LINE)]
-        y_blk = lax.psum_scatter(y_part, "tp", scatter_dimension=0, axis_index_groups=columns, tiled=True).astype(BF16)
+        y_sum = lax.psum_scatter(y_part, "tp", scatter_dimension=0, axis_index_groups=columns, tiled=True)
         shard_buf = pltpu.VMEM((2 * n_sh, half_rows, width), BF16)
-        dq, dkv = attention_call(
+        w_slot = jax.ShapeDtypeStruct(w_shared.shape, BF16)
+        dq, dkv, w_prev, w_next, w_far = attention_call(
             functools.partial(backward_kernel, n_sh, heads, dim), "attn_bwd", 1, 7 * tile_flops // 2,
-            [VMEM_SPEC, VMEM_SPEC, VMEM_SPEC, ANY_SPEC], [VMEM_SPEC, VMEM_SPEC],
-            [jax.ShapeDtypeStruct((2, half_rows, width), BF16), jax.ShapeDtypeStruct((2, half_rows, 2 * width), BF16)],
+            [VMEM_SPEC, VMEM_SPEC, VMEM_SPEC, ANY_SPEC, ANY_SPEC], [VMEM_SPEC, VMEM_SPEC] + [ANY_SPEC] * 3,
+            [jax.ShapeDtypeStruct((2, half_rows, width), BF16), jax.ShapeDtypeStruct((2, half_rows, 2 * width), BF16)] + [w_slot] * 3,
             [pltpu.VMEM(kv_all_shape, BF16), shard_buf, shard_buf, pltpu.VMEM((2 * n_sh, 8, half_rows), F32),
-             acc, acc, acc, acc, acc, dma((27,)), dma((27,)), dma((4,))],
-        )(q, d_o, stats, kv_all)
+             acc, acc, acc, acc, acc, dma((27,)), dma((27,)), dma((8,)), dma((8,)), dma((4,))],
+        )(q, d_o, stats, kv_all, w_shared)
 
         dq_flat = dq.reshape(n_rows, width)
         dkv_flat = dkv.reshape(n_rows, 2 * width)
         d_all = jnp.concatenate([dq_flat, dkv_flat], axis=1)
-        w_all = jnp.concatenate([wq, wkv], axis=1)
-        dx_part = dot_t(d_all, w_all)
-        dx_blk = lax.psum_scatter(dx_part, "tp", scatter_dimension=0, tiled=True).astype(BF16)
+        dx_first = dot_t(d_all, w_all[:n_cols])
+        dx_first, dq, dkv, y_sum = lax.optimization_barrier((dx_first, dq, dkv, y_sum))
+        dx_first = lax.psum_scatter(dx_first, "tp", scatter_dimension=0, tiled=True)
+        d_rows = pl.pallas_call(
+            grad_rows_kernel,
+            name="grad_rows",
+            out_shape=[jax.ShapeDtypeStruct((n_z, blk_rows, 3 * width), BF16)] * LINE,
+            in_specs=[VMEM_SPEC] * 2,
+            out_specs=[VMEM_SPEC] * LINE,
+            scratch_shapes=[pltpu.VMEM((LINE - 1, n_z, blk_rows, width), BF16), pltpu.VMEM((LINE - 1, n_z, blk_rows, 2 * width), BF16),
+                            dma((2 * LINE - 2,)), dma((2 * LINE - 2,))],
+            compiler_params=pltpu.CompilerParams(collective_id=3, has_side_effects=True),
+        )(dq.reshape(n_z, LINE, blk_rows, width), dkv.reshape(n_z, LINE, blk_rows, 2 * width))
+        d_rows = [part.reshape(n_z * blk_rows, 3 * width) for part in d_rows]
+        dx_second = dot_t(d_rows[0], w_shared)
+        for slot, w_part in enumerate((w_prev, w_next, w_far)):
+            dx_second = dx_second + dot_t(d_rows[slot + 1], w_part)
+        dq_flat = dq.reshape(n_rows, width)
+        dkv_flat = dkv.reshape(n_rows, 2 * width)
 
         def weight_grad(lhs, rhs, shape):
             return lax.dot_general(lhs, rhs, ROWS_CONTRACT, preferred_element_type=F32).astype(BF16).reshape(shape)[None]
@@ -479,7 +634,10 @@
         grad_wq = weight_grad(x_rows, dq_flat, (model_dim, heads, dim))
         grad_wk = weight_grad(x_rows, dkv_flat[:, :width], (model_dim, heads, dim))
         grad_wv = weight_grad(x_rows, dkv_flat[:, width:], (model_dim, heads, dim))
-        return y_blk, dx_blk, grad_wq, grad_wk, grad_wv, grad_wo
+        dx_second, dx_first, grad_wo, grad_wq, grad_wk = lax.optimization_barrier((dx_second, dx_first, grad_wo, grad_wq, grad_wk))
+        dx_second = lax.psum_scatter(dx_second, "tp", scatter_dimension=0, axis_index_groups=columns, tiled=True)
+        dx_blk = jnp.concatenate([dx_first, dx_second], axis=1).astype(BF16)
+        return y_sum.astype(BF16), dx_blk, grad_wq, grad_wk, grad_wv, grad_wo
 
     return jax.shard_map(device_fn, mesh=mesh,
                          in_specs=(ROW_SPEC, HEAD_SPEC, HEAD_SPEC, HEAD_SPEC, OUT_W_SPEC, ROW_SPEC),

time: 391 us -> 395 us (1.010)
  waiting for transfers between devices: 150 us -> 37.1 us
  Pallas kernels: 132 us -> 232 us
  local copies, waits for them, and re-layouts: 19 us -> 29.8 us
  matrix products: 67.3 us -> 71.9 us
    pallas_call x0 -> x2, Pallas kernels: none -> 92 us  [the longest x1 51.6 us: gather_rows(): pl.pallas_call(gather_rows_kernel, name='gather_rows', out_shape=jax.Shap...]
    all_gather x1 -> x0, waiting for transfers between devices: 69.8 us -> none  [device_fn(): x_rows = lax.all_gather(x_blk, 'tp', axis=0, tiled=True)]
    reduce_scatter x1 -> x2, waiting for transfers between devices: 69.8 us -> 30.5 us  [the longest x1 23.3 us: device_fn(): dx_first = lax.psum_scatter(dx_first, 'tp', scatter_dimension=0, tiled=True)]
    unnamed x14 -> x37, local copies, waits for them, and re-layouts: 12.6 us -> 26.4 us
    pallas_call x1, Pallas kernels: 52 us -> 60 us  [device_fn(): attention_call(functools.partial(backward_kernel, n_sh, heads, dim), 'att...]
    dot_general x2 -> x6, matrix products: 19.2 us -> 23.8 us  [dot_t(): return lax.dot_general(lhs, rhs, COLS_CONTRACT, preferred_element_type=F32)]
    reshape x1, local copies, waits for them, and re-layouts: 4.9 us -> 0.91 us  [device_fn(): w_value.reshape(model_dim, width)]
  transfers between devices with their start and end apart: 4 -> 4, of which waited for: 3 -> 3; matrix products, arithmetic and copies ran while one was open for 19% -> 20% of each run, Pallas kernels for 31% -> 43%
where the time goes in v2:
time: 395 us; the launch traced here: 388 us
  Pallas kernels  232 us (59%)
  matrix products  71.9 us (18%)
  waiting for transfers between devices  37.1 us (9%)
  local copies, waits for them, and re-layouts  29.8 us (8%)
  between operations  14.2 us (4%)
    pallas_call x1, Pallas kernels, device_fn(): attention_call(functools.partial(forward_kernel, n_sh, heads, dim), 'attn...  68.1 us
    pallas_call x1, Pallas kernels, device_fn(): attention_call(functools.partial(backward_kernel, n_sh, heads, dim), 'att...  60 us
    pallas_call x1, Pallas kernels, gather_rows(): pl.pallas_call(gather_rows_kernel, name='gather_rows', out_shape=jax.Shap...  51.6 us
    pallas_call x1, Pallas kernels, device_fn(): pl.pallas_call(grad_rows_kernel, name='grad_rows', out_shape=[jax.ShapeDt...  40.5 us
    dot_general x4, matrix products, weight_grad(): lax.dot_general(lhs, rhs, ROWS_CONTRACT, preferred_element_type=F32)  27.4 us
    unnamed x37, local copies, waits for them, and re-layouts  26.4 us
    dot_general x6, matrix products, dot_t(): return lax.dot_general(lhs, rhs, COLS_CONTRACT, preferred_element_type=F32)  23.8 us
    reduce_scatter x1, waiting for transfers between devices, device_fn(): dx_first = lax.psum_scatter(dx_first, 'tp', scatter_dimension=0, tiled=True)  23.3 us
  transfers between devices with their start and end apart: 4, of which 3 were waited for; matrix products, arithmetic and copies ran while one was open for 20% of the time, Pallas kernels for 43%

profile of v2, /device:TPU:0, one launch (start us, length us, event | category | flops | bytes accessed | tf_op | source)
XLA Modules:
  0.0 388.4 jit_solution(9464395295027921815)
XLA Ops:
  7.2 51.6 %gather_rows.1 = bf16[16,64,4096]{2,1,0:T(8,128)(2,1)} custom-call(bf16[64,4096]{1,0:T(8,128)(2,1)} %x_ref.1), custom_call_target="tpu_custom_call" | custom-call | tf_op jit(solution)/shard_map/gather_rows/pallas_call | solution.py:517
  58.9 7.3 %fusion.15 = bf16[1024,256]{1,0:T(8,128)(2,1)} fusion(bf16[1024,4096]{1,0:T(8,128)(2,1)} %bitcast.63, bf16[512,8,2,128]{3,2,1,0:T(2,128)(2,1)} %bitcast.75), kind=kOutput, calls=%fused_computation.25 | convolution fusion | flops 2147745792 | bytes 11010048 | tf_op jit(solution)/shard_map/dot_general | solution.py:28
  67.1 2.5 copy-done
  69.5 5.5 %fusion.12 = bf16[1024,512]{1,0:T(8,128)(2,1)} fusion(bf16[1024,4096]{1,0:T(8,128)(2,1)S(1)} %bitcast.67, bf16[4096,256]{1,0:T(8,128)(2,1)S(1)} %get-tuple-element.76, bf16[4096,256]{1,0:T(8,128)(2,1)S(1)} %get-tuple-element.77), kind=kOutput, calls=%fused_computation.24 | convolution fusion | flops 4303880192 | bytes 13631488 | tf_op jit(solution)/shard_map/dot_general | solution.py:28
  75.0 68.1 %attn_fwd.1 = (bf16[2,512,256]{2,1,0:T(8,128)(2,1)}, f32[2,2,512]{2,1,0:T(2,128)}, bf16[16,512,512]{2,1,0:T(8,128)(2,1)}, bf16[4,256,4096]{2,1,0:T(8,128)(2,1)}) custom-call(bf16[2,512,256]{2,1,0:T(8,128)(2,1)} %bitcast.98, bf16[2,512,512]{2,1,0:T(8,128)(2,1)} %bitcast.97, bf16[256,4096]{1,0:T(8,128)(2,1)} %bitcast.92), custom_call_target="tpu_custom_call" | custom-call | flops 9126805504 | bytes 10485760 | tf_op jit(solution)/shard_map/attn_fwd/pallas_call | solution.py:569
  143.1 6.5 %all-gather.2.cloned.1.call-done = bf16[1024,4096]{1,0:T(8,128)(2,1)} async-done(((bf16[64,4096]{1,0:T(8,128)(2,1)}), bf16[1024,4096]{1,0:T(8,128)(2,1)}) %all-gather.2.cloned.1.call-update) | async-done | bytes 8388624 | tf_op jit(solution)/shard_map/all_gather | solution.py:558
  149.6 7.1 %convolution_convert_fusion.4 = bf16[1024,256]{1,0:T(8,128)(2,1)} fusion(bf16[1024,4096]{1,0:T(8,128)(2,1)} %all-gather.2.cloned.1.call-done, bf16[256,4096]{1,0:T(8,128)(2,1)} %bitcast.93), kind=kOutput, calls=%fused_computation.26 | convolution fusion | flops 2147745792 | bytes 11010048 | tf_op jit(solution)/shard_map/dot_general | solution.py:24
  156.7 12.1 %attn_stats.1 = (f32[2,8,512]{2,1,0:T(8,128)}, bf16[4,64,1024]{2,1,0:T(8,128)(2,1)}) custom-call(bf16[4,4,64,256]{3,2,1,0:T(8,128)(2,1)} %bitcast.72, bf16[2,512,256]{2,1,0:T(8,128)(2,1)} %bitcast.87, f32[2,2,512]{2,1,0:T(2,128)} %get-tuple-element.42.lse_ref), custom_call_target="tpu_custom_call" | custom-call | tf_op jit(solution)/shard_map/attn_stats/pallas_call | solution.py:584
  168.8 8.0 %fusion.24 = f32[256,4096]{1,0:T(8,128)} fusion(bf16[256,1024]{1,0:T(8,128)(2,1)} %bitcast.94, bf16[1024,4096]{1,0:T(8,128)(2,1)} %bitcast.96), kind=kOutput, calls=%fused_computation.34 | convolution fusion | flops 2147483648 | bytes 13107200 | tf_op jit(solution)/shard_map/dot_general | solution.py:28
  180.9 2.0 slice.16.w_ref
  184.6 60.0 %attn_bwd.1 = (bf16[2,512,256]{2,1,0:T(8,128)(2,1)}, bf16[2,512,512]{2,1,0:T(8,128)(2,1)}, bf16[2048,768]{1,0:T(8,128)(2,1)}, bf16[2048,768]{1,0:T(8,128)(2,1)}, bf16[2048,768]{1,0:T(8,128)(2,1)}) custom-call(bf16[2,512,256]{2,1,0:T(8,128)(2,1)} %bitcast.99, bf16[2,512,256]{2,1,0:T(8,128)(2,1)} %bitcast.88, f32[2,8,512]{2,1,0:T(8,128)} %get-tuple-element.46.st_ref, ...), custom_call_target="tpu_custom_call" | custom-call | flops 15971909632 | bytes 10485760 | tf_op jit(solution)/shard_map/attn_bwd/pallas_call | solution.py:599
  244.6 9.1 %fusion.4 = f32[1024,2048]{1,0:T(8,128)} fusion(bf16[4096,768]{1,0:T(8,128)(2,1)} %copy-done.4, bf16[1024,512]{1,0:T(8,128)(2,1)} %bitcast.80, bf16[1024,256]{1,0:T(8,128)(2,1)} %bitcast.84), kind=kOutput, calls=%fused_computation.8 | convolution fusion | flops 3224371200 | bytes 13107200 | tf_op jit(solution)/shard_map/dot_general | solution.py:24
  254.7 7.1 %convolution_convert_fusion.3 = bf16[256,4096]{1,0:T(8,128)(2,1)} fusion(bf16[1024,256]{1,0:T(8,128)(2,1)S(1)} %bitcast.73, bf16[1024,4096]{1,0:T(8,128)(2,1)} %all-gather.2.cloned.1.call-done), kind=kOutput, calls=%fused_computation.3 | convolution fusion | flops 2148532224 | bytes 11010048 | tf_op jit(solution)/shard_map/dot_general | solution.py:631
  261.8 40.5 %grad_rows.1 = (bf16[4,64,768]{2,1,0:T(8,128)(2,1)}, bf16[4,64,768]{2,1,0:T(8,128)(2,1)}, bf16[4,64,768]{2,1,0:T(8,128)(2,1)}, bf16[4,64,768]{2,1,0:T(8,128)(2,1)}) custom-call(bf16[4,4,64,256]{3,2,1,0:T(8,128)(2,1)} %bitcast.85, bf16[4,4,64,512]{3,2,1,0:T(8,128)(2,1)} %bitcast.81), custom_call_target="tpu_custom_call" | custom-call | tf_op jit(solution)/shard_map/grad_rows/pallas_call | solution.py:613
  302.3 3.2 fusion.22
  309.4 2.4 convolution_add_fusion
  311.8 5.9 %convolution_convert_fusion.2 = bf16[4096,256]{0,1:T(8,128)(2,1)S(1)} fusion(bf16[1024,4096]{1,0:T(8,128)(2,1)} %bitcast.64, bf16[1024,256]{1,0:T(8,128)(2,1)S(1)} %bitcast.86), kind=kOutput, calls=%fused_computation.2 | convolution fusion | flops 2148532224 | bytes 11010048 | tf_op jit(solution)/shard_map/dot_general | solution.py:631
  317.7 7.2 %convolution_convert_fusion.1 = bf16[4096,256]{0,1:T(8,128)(2,1)} fusion(bf16[1024,4096]{1,0:T(8,128)(2,1)} %bitcast.65, bf16[1024,512]{1,0:T(8,128)(2,1)S(1)} %bitcast.83), kind=kOutput, calls=%fused_computation.1 | convolution fusion | flops 2148532224 | bytes 11010048 | tf_op jit(solution)/shard_map/dot_general | solution.py:631
  324.9 23.3 %reduce-scatter.6.cloned.1.call-done = f32[64,2048]{1,0:T(8,128)} async-done(((f32[1024,2048]{1,0:T(8,128)}), f32[64,2048]{1,0:T(8,128)}) %reduce-scatter.6.cloned.1.call-update) | async-done | bytes 524304 | tf_op jit(solution)/shard_map/reduce_scatter | solution.py:612
  349.1 7.2 %convolution_convert_fusion = bf16[4096,256]{0,1:T(8,128)(2,1)} fusion(bf16[1024,4096]{1,0:T(8,128)(2,1)} %bitcast.66, bf16[1024,512]{1,0:T(8,128)(2,1)} %bitcast.82), kind=kOutput, calls=%fused_computation | convolution fusion | flops 2148532224 | bytes 11010048 | tf_op jit(solution)/shard_map/dot_general | solution.py:631
  356.3 6.2 %copy.14 = bf16[1,4096,2,128]{3,2,1,0:T(2,128)(2,1)} copy(bf16[1,4096,2,128]{1,3,2,0:T(8,128)(2,1)} %bitcast.79) | data formatting | bytes 4194304
  362.5 3.8 copy.12
  366.3 6.2 %copy.13 = bf16[1,4096,2,128]{3,2,1,0:T(2,128)(2,1)} copy(bf16[1,4096,2,128]{1,3,2,0:T(8,128)(2,1)} %bitcast.78) | data formatting | bytes 4194304
  372.5 7.2 %reduce-scatter.8.cloned.1.call-done = f32[64,2048]{1,0:T(8,128)} async-done(((f32[256,2048]{1,0:T(8,128)}), f32[64,2048]{1,0:T(8,128)}) %reduce-scatter.8.cloned.1.call-update) | async-done | bytes 524304 | tf_op jit(solution)/shard_map/reduce_scatter | solution.py:638
  (50 shorter events, 14.5 us)
Async XLA Ops:
  7.2 142.4 %all-gather.2.cloned.1.call-start = ((), (), s32[]{:S(2)}) async-start(), calls=%async_computation.3 | async-start | bytes 8912896 | tf_op jit(solution)/shard_map/all_gather | solution.py:558
  58.8 194.9 %reduce-scatter.4.cloned.1.call-start = ((), (), s32[]{:S(2)}) async-start(), calls=%async_computation.4 | async-start | bytes 5242880 | tf_op jit(solution)/shard_map/reduce_scatter | solution.py:596
  58.9 7.3 %copy-start.1 = (bf16[4096,2,128]{2,1,0:T(2,128)(2,1)S(1)}, bf16[4096,2,128]{2,1,0:T(2,128)(2,1)}, u32[]{:S(2)}) copy-start(bf16[4096,2,128]{2,1,0:T(2,128)(2,1)} %param.8) | copy-start | bytes 6291460
  58.9 7.3 %copy-start.2 = (bf16[4096,2,128]{2,1,0:T(2,128)(2,1)S(1)}, bf16[4096,2,128]{2,1,0:T(2,128)(2,1)}, u32[]{:S(2)}) copy-start(bf16[4096,2,128]{2,1,0:T(2,128)(2,1)} %param.9) | copy-start | bytes 6291460
  66.1 3.4 copy-start
  176.8 171.4 %reduce-scatter.6.cloned.1.call-start = ((), (), s32[]{:S(2)}) async-start(), calls=%async_computation.5 | async-start | bytes 8912896 | tf_op jit(solution)/shard_map/reduce_scatter | solution.py:612
  178.8 1.6 copy-start.3
  180.9 3.7 copy-start.4
  253.7 1.0 copy-start.8
  253.7 126.0 %reduce-scatter.8.cloned.1.call-start = ((), (), s32[]{:S(2)}) async-start(), calls=%async_computation.6 | async-start | bytes 2621440 | tf_op jit(solution)/shard_map/reduce_scatter | solution.py:638
  302.3 3.2 copy-start.7
  302.3 3.2 copy-start.15
  305.5 1.9 copy-start.6
  305.5 1.9 copy-start.14
  307.4 1.9 copy-start.5
  307.4 1.9 copy-start.13
  309.4 2.4 copy-start.11
  311.8 5.9 %copy-start.10 = (bf16[2,512,512]{2,1,0:T(8,128)(2,1)S(1)}, bf16[2,512,512]{2,1,0:T(8,128)(2,1)}, u32[]{:S(2)}) copy-start(bf16[2,512,512]{2,1,0:T(8,128)(2,1)} %get-tuple-element.56) | copy-start | bytes 3145732
  317.7 30.6 %copy-start.9 = (f32[64,4096]{1,0:T(8,128)S(1)}, f32[64,4096]{1,0:T(8,128)}, u32[]{:S(2)}) copy-start(f32[64,4096]{1,0:T(8,128)} %reduce-scatter.4.cloned.1.call-done) | copy-start | bytes 3145732
  356.3 6.2 %copy-start.12 = (f32[64,2048]{1,0:T(8,128)S(1)}, f32[64,2048]{1,0:T(8,128)}, u32[]{:S(2)}) copy-start(f32[64,2048]{1,0:T(8,128)} %reduce-scatter.6.cloned.1.call-done) | copy-start | bytes 1572868
Sparse Core Ops, SparseCore 0:
  58.9 90.5 all-gather.1
  176.9 45.9 reduce-scatter.3
  253.8 94.3 reduce-scatter.5
  350.5 29.1 reduce-scatter.7

commit v3 on v1

--- a/solution.py
+++ b/solution.py
@@ -393,6 +393,100 @@
     wait_sends()
 
 
+def gather_rows_kernel(x_ref, all_ref, sends, recvs, sem):
+    tp_idx = lax.axis_index("tp")
+    pos = (tp_idx // LINE, lax.rem(tp_idx, LINE))
+    half_rows = x_ref.shape[0] // 2
+    quarter = half_rows // 2
+
+    def block(axis, fast, slow):
+        off = (slow, fast) if axis == 1 else (fast, slow)
+        z_idx, y_idx = [lax.rem(base + shift + LINE, LINE) for base, shift in zip(pos, off)]
+        return LINE * z_idx + y_idx
+
+    barrier = pltpu.get_barrier_semaphore()
+    for axis in range(2):
+        for shift in (1, -1):
+            pl.semaphore_signal(barrier, inc=1, device_id={"tp": block(axis, shift, 0)}, device_id_type=pl.DeviceIdType.MESH)
+    pl.semaphore_wait(barrier, 4)
+
+    own = pltpu.make_async_copy(x_ref, all_ref.at[block(1, 0, 0)], sem.at[0])
+    own.start()
+    table = {}
+    for colour in range(2):
+        axis = 1 - colour
+        base = colour * half_rows
+        whole, low, high = (base, half_rows), (base, quarter), (base + quarter, quarter)
+
+        def add(name, fast, slow, rows, along_fast, shift):
+            idx = len(table)
+            span = pl.ds(*rows)
+            blk = block(axis, fast, slow)
+            src = x_ref.at[span] if fast == 0 and slow == 0 else all_ref.at[blk, span]
+            target = block(axis, shift, 0) if along_fast else block(axis, 0, shift)
+            table[colour, name] = pltpu.make_async_remote_copy(
+                src_ref=src, dst_ref=all_ref.at[blk, span], send_sem=sends.at[idx], recv_sem=recvs.at[idx],
+                device_id={"tp": target}, device_id_type=pl.DeviceIdType.MESH)
+
+        add("prev", 0, 0, whole, True, 1)
+        add("next", 0, 0, whole, True, -1)
+        add("far_lo", -1, 0, low, True, 1)
+        add("far_hi", 1, 0, high, True, -1)
+        for fast in (0, -1, 1, 2):
+            add(("prev", fast), fast, 0, whole, False, 1)
+            add(("next", fast), fast, 0, whole, False, -1)
+            add(("far_lo", fast), fast, -1, low, False, 1)
+            add(("far_hi", fast), fast, 1, high, False, -1)
+
+    def start(*names):
+        for name in names:
+            for colour in range(2):
+                table[colour, name].start()
+
+    def wait(*names):
+        for name in names:
+            for colour in range(2):
+                table[colour, name].wait_recv()
+
+    start("prev", "next", ("prev", 0), ("next", 0))
+    wait("prev")
+    start("far_lo", ("prev", -1), ("next", -1))
+    wait("next")
+    start("far_hi", ("prev", 1), ("next", 1))
+    wait(("prev", 0))
+    start(("far_lo", 0))
+    wait(("next", 0))
+    start(("far_hi", 0))
+    wait("far_lo", "far_hi")
+    start(("prev", 2), ("next", 2))
+    for fast in (-1, 1, 2):
+        wait(("prev", fast))
+        start(("far_lo", fast))
+        wait(("next", fast))
+        start(("far_hi", fast))
+    for fast in (0, -1, 1, 2):
+        wait(("far_lo", fast), ("far_hi", fast))
+    own.wait()
+    for copy in table.values():
+        copy.wait_send()
+
+
+def gather_rows(x_blk, n_tp):
+    rows, cols = x_blk.shape
+    if n_tp != LINE * LINE:
+        return lax.all_gather(x_blk, "tp", axis=0, tiled=True)
+    gathered = pl.pallas_call(
+        gather_rows_kernel,
+        name="gather_rows",
+        out_shape=jax.ShapeDtypeStruct((n_tp, rows, cols), x_blk.dtype),
+        in_specs=[VMEM_SPEC],
+        out_specs=ANY_SPEC,
+        scratch_shapes=[pltpu.SemaphoreType.DMA((40,)), pltpu.SemaphoreType.DMA((40,)), pltpu.SemaphoreType.DMA((1,))],
+        compiler_params=pltpu.CompilerParams(collective_id=4, has_side_effects=True),
+    )(x_blk)
+    return gathered.reshape(n_tp * rows, cols)
+
+
 VMEM_SPEC = pl.BlockSpec(memory_space=pltpu.VMEM)
 ANY_SPEC = pl.BlockSpec(memory_space=pl.ANY)
 
@@ -420,7 +514,8 @@
         wkv = jnp.concatenate([w_key.reshape(model_dim, width), w_value.reshape(model_dim, width)], axis=1)
         wo = w_out.reshape(width, model_dim)
 
-        x_rows = lax.all_gather(x_blk, "tp", axis=0, tiled=True)
+        x_rows = gather_rows(x_blk, mesh.shape["tp"])
+        x_rows, dy_blk = lax.optimization_barrier((x_rows, dy_blk))
         dy_rows = lax.all_gather(dy_blk, "tp", axis=0, tiled=True)
         n_rows = x_rows.shape[0]
         half_rows = n_rows // 2
@@ -440,6 +535,9 @@
             [pltpu.VMEM(kv_all_shape, BF16), acc, acc, acc, dma((9,)), dma((9,)), dma((8,)), dma((8,)), dma((2,))],
         )(q, kv, wo)
         o_flat = o.reshape(n_rows, width)
+        lse, *late_weights = lax.optimization_barrier((lse, w_query, w_key, w_value))
+        w_all = jnp.concatenate([w_late.reshape(model_dim, width) for w_late in late_weights], axis=1)
+        dy_rows, w_all = lax.optimization_barrier((dy_rows, w_all))
         d_o = dot_t(dy_rows, wo).astype(BF16).reshape(2, half_rows, width)
         n_z = mesh.shape["tp"] // LINE
         blk_rows = n_rows // mesh.shape["tp"]
@@ -468,7 +566,6 @@
         dq_flat = dq.reshape(n_rows, width)
         dkv_flat = dkv.reshape(n_rows, 2 * width)
         d_all = jnp.concatenate([dq_flat, dkv_flat], axis=1)
-        w_all = jnp.concatenate([wq, wkv], axis=1)
         dx_part = dot_t(d_all, w_all)
         dx_blk = lax.psum_scatter(dx_part, "tp", scatter_dimension=0, tiled=True).astype(BF16)
 

time: 391 us -> 364 us (0.931)
  waiting for transfers between devices: 150 us -> 71 us
  Pallas kernels: 132 us -> 184 us
    all_gather x1 -> x0, waiting for transfers between devices: 69.8 us -> none  [device_fn(): x_rows = lax.all_gather(x_blk, 'tp', axis=0, tiled=True)]
    pallas_call x0 -> x1, Pallas kernels: none -> 51.6 us  [gather_rows(): pl.pallas_call(gather_rows_kernel, name='gather_rows', out_shape=jax.Shap...]
    all_gather x1, waiting for transfers between devices: 8.94 us -> 1.29 us  [device_fn(): dy_rows = lax.all_gather(dy_blk, 'tp', axis=0, tiled=True)]
    unnamed x14 -> x22, local copies, waits for them, and re-layouts: 12.6 us -> 16.9 us
    reshape x1, local copies, waits for them, and re-layouts: 4.9 us -> 0.67 us  [device_fn(): w_value.reshape(model_dim, width)]
  transfers between devices with their start and end apart: 4 -> 3, of which waited for: 3 -> 2; matrix products, arithmetic and copies ran while one was open for 19% -> 19% of each run, Pallas kernels for 31% -> 33%
where the time goes in v3:
time: 364 us; the launch traced here: 358 us
  Pallas kernels  184 us (51%)
  waiting for transfers between devices  71 us (20%)
  matrix products  64.3 us (18%)
  local copies, waits for them, and re-layouts  17.6 us (5%)
  between operations  14.1 us (4%)
  other arithmetic  7.44 us (2%)
    reduce_scatter x1, waiting for transfers between devices, device_fn(): lax.psum_scatter(dx_part, 'tp', scatter_dimension=0, tiled=True)  69.6 us
    pallas_call x1, Pallas kernels, device_fn(): attention_call(functools.partial(forward_kernel, n_sh, heads, dim), 'attn...  68.1 us
    pallas_call x1, Pallas kernels, device_fn(): attention_call(functools.partial(backward_kernel, n_sh, heads, dim), 'att...  51.8 us
    pallas_call x1, Pallas kernels, gather_rows(): pl.pallas_call(gather_rows_kernel, name='gather_rows', out_shape=jax.Shap...  51.6 us
    dot_general x4, matrix products, weight_grad(): lax.dot_general(lhs, rhs, ROWS_CONTRACT, preferred_element_type=F32)  24.5 us
    dot_general x3, matrix products, dot_n(): return jnp.dot(lhs, rhs, preferred_element_type=F32)  20.6 us
    dot_general x2, matrix products, dot_t(): return lax.dot_general(lhs, rhs, COLS_CONTRACT, preferred_element_type=F32)  19.2 us
    unnamed x22, local copies, waits for them, and re-layouts  16.9 us
  transfers between devices with their start and end apart: 3, of which 2 were waited for; matrix products, arithmetic and copies ran while one was open for 19% of the time, Pallas kernels for 33%

profile of v3, /device:TPU:0, one launch (start us, length us, event | category | flops | bytes accessed | tf_op | source)
XLA Modules:
  0.0 358.1 jit_solution(984047408588099906)
XLA Ops:
  7.2 51.6 %gather_rows.1 = bf16[16,64,4096]{2,1,0:T(8,128)(2,1)} custom-call(bf16[64,4096]{1,0:T(8,128)(2,1)} %x_ref.1), custom_call_target="tpu_custom_call" | custom-call | tf_op jit(solution)/shard_map/gather_rows/pallas_call | solution.py:478
  58.9 7.3 %fusion.14 = bf16[1024,256]{1,0:T(8,128)(2,1)} fusion(bf16[1024,4096]{1,0:T(8,128)(2,1)} %bitcast.52, bf16[512,8,2,128]{3,2,1,0:T(2,128)(2,1)} %bitcast.67), kind=kOutput, calls=%fused_computation.22 | convolution fusion | flops 2147745792 | bytes 11010048 | tf_op jit(solution)/shard_map/dot_general | solution.py:28
  66.8 2.7 copy-done
  69.5 5.5 %fusion.11 = bf16[1024,512]{1,0:T(8,128)(2,1)} fusion(bf16[1024,4096]{1,0:T(8,128)(2,1)S(1)} %bitcast.56, bf16[4096,256]{1,0:T(8,128)(2,1)S(1)} %get-tuple-element.48, bf16[4096,256]{1,0:T(8,128)(2,1)S(1)} %get-tuple-element.49), kind=kOutput, calls=%fused_computation.21 | convolution fusion | flops 4303880192 | bytes 13631488 | tf_op jit(solution)/shard_map/dot_general | solution.py:28
  75.0 68.1 %attn_fwd.1 = (bf16[2,512,256]{2,1,0:T(8,128)(2,1)}, f32[2,2,512]{2,1,0:T(2,128)}, bf16[16,512,512]{2,1,0:T(8,128)(2,1)}, bf16[4,256,4096]{2,1,0:T(8,128)(2,1)}) custom-call(bf16[2,512,256]{2,1,0:T(8,128)(2,1)} %bitcast.82, bf16[2,512,512]{2,1,0:T(8,128)(2,1)} %bitcast.81, bf16[256,4096]{1,0:T(8,128)(2,1)} %bitcast.74), custom_call_target="tpu_custom_call" | custom-call | flops 9126805504 | bytes 10485760 | tf_op jit(solution)/shard_map/attn_fwd/pallas_call | solution.py:530
  143.7 1.0 copy-done.4
  145.0 3.3 pad_maximum_fusion
  148.3 1.3 all-gather.2.cloned.1.call-done
  149.6 6.5 %convolution_convert_fusion.4 = bf16[1024,256]{1,0:T(8,128)(2,1)} fusion(bf16[1024,4096]{1,0:T(8,128)(2,1)} %all-gather.2.cloned.1.call-done, bf16[256,4096]{1,0:T(8,128)(2,1)S(1)} %bitcast.75), kind=kOutput, calls=%fused_computation.23 | convolution fusion | flops 2147745792 | bytes 11010048 | tf_op jit(solution)/shard_map/dot_general | solution.py:24
  156.1 12.1 %attn_stats.1 = (f32[2,8,512]{2,1,0:T(8,128)}, bf16[4,64,1024]{2,1,0:T(8,128)(2,1)}) custom-call(bf16[4,4,64,256]{3,2,1,0:T(8,128)(2,1)} %bitcast.64, bf16[2,512,256]{2,1,0:T(8,128)(2,1)} %bitcast.72, f32[2,2,512]{2,1,0:T(2,128)} %get-tuple-element.32.lse_ref), custom_call_target="tpu_custom_call" | custom-call | tf_op jit(solution)/shard_map/attn_stats/pallas_call | solution.py:544
  168.2 7.9 %fusion.21 = f32[256,4096]{1,0:T(8,128)} fusion(bf16[256,1024]{1,0:T(8,128)(2,1)} %bitcast.76, bf16[1024,4096]{1,0:T(8,128)(2,1)} %bitcast.77), kind=kOutput, calls=%fused_computation.28 | convolution fusion | flops 2147483648 | bytes 13107200 | tf_op jit(solution)/shard_map/dot_general | solution.py:28
  176.2 51.8 %attn_bwd.1 = (bf16[2,512,256]{2,1,0:T(8,128)(2,1)}, bf16[2,512,512]{2,1,0:T(8,128)(2,1)}) custom-call(bf16[2,512,256]{2,1,0:T(8,128)(2,1)} %bitcast.83, bf16[2,512,256]{2,1,0:T(8,128)(2,1)} %bitcast.73, f32[2,8,512]{2,1,0:T(8,128)} %get-tuple-element.37.st_ref, bf16[16,512,512]{2,1,0:T(8,128)(2,1)} %get-tuple-element.38.all_ref), custom_call_target="tpu_custom_call" | custom-call | flops 15971909632 | bytes 10485760 | tf_op jit(solution)/shard_map/attn_bwd/pallas_call | solution.py:558
  228.0 12.7 %fusion.7 = f32[1024,4096]{1,0:T(8,128)} fusion(bf16[4096,768]{1,0:T(8,128)(2,1)} %pad_maximum_fusion, bf16[1024,512]{1,0:T(8,128)(2,1)} %bitcast.78, bf16[1024,256]{1,0:T(8,128)(2,1)} %bitcast.84), kind=kOutput, calls=%fused_computation.17 | convolution fusion | flops 6445596672 | bytes 24641536 | tf_op jit(solution)/shard_map/dot_general | solution.py:24
  240.7 1.0 copy-done.7
  241.7 5.8 %convolution_convert_fusion.3 = bf16[4096,256]{0,1:T(8,128)(2,1)S(1)} fusion(bf16[1024,4096]{1,0:T(8,128)(2,1)} %bitcast.53, bf16[1024,256]{1,0:T(8,128)(2,1)S(1)} %bitcast.85), kind=kOutput, calls=%fused_computation.4 | convolution fusion | flops 2148532224 | bytes 11010048 | tf_op jit(solution)/shard_map/dot_general | solution.py:573
  247.5 3.8 %copy.12 = bf16[1,4096,2,128]{3,2,1,0:T(2,128)(2,1)} copy(bf16[1,4096,2,128]{1,3,2,0:T(8,128)(2,1)S(1)} %bitcast.70) | data formatting | bytes 4194304
  251.3 5.8 %convolution_convert_fusion.2 = bf16[4096,256]{0,1:T(8,128)(2,1)S(1)} fusion(bf16[1024,4096]{1,0:T(8,128)(2,1)} %bitcast.54, bf16[1024,512]{1,0:T(8,128)(2,1)S(1)} %bitcast.80), kind=kOutput, calls=%fused_computation.3 | convolution fusion | flops 2148532224 | bytes 11010048 | tf_op jit(solution)/shard_map/dot_general | solution.py:573
  257.1 3.8 %copy.13 = bf16[1,4096,2,128]{3,2,1,0:T(2,128)(2,1)} copy(bf16[1,4096,2,128]{1,3,2,0:T(8,128)(2,1)S(1)} %bitcast.71) | data formatting | bytes 4194304
  260.9 5.8 %convolution_convert_fusion.1 = bf16[4096,256]{0,1:T(8,128)(2,1)S(1)} fusion(bf16[1024,4096]{1,0:T(8,128)(2,1)} %bitcast.55, bf16[1024,512]{1,0:T(8,128)(2,1)} %bitcast.79), kind=kOutput, calls=%fused_computation.2 | convolution fusion | flops 2148532224 | bytes 11010048 | tf_op jit(solution)/shard_map/dot_general | solution.py:573
  266.7 3.8 %copy.14 = bf16[1,4096,2,128]{3,2,1,0:T(2,128)(2,1)} copy(bf16[1,4096,2,128]{1,3,2,0:T(8,128)(2,1)S(1)} %bitcast.69) | data formatting | bytes 4194304
  270.5 7.1 %convolution_convert_fusion = bf16[256,4096]{1,0:T(8,128)(2,1)} fusion(bf16[1024,256]{1,0:T(8,128)(2,1)S(1)} %bitcast.65, bf16[1024,4096]{1,0:T(8,128)(2,1)} %all-gather.2.cloned.1.call-done), kind=kOutput, calls=%fused_computation.1 | convolution fusion | flops 2148532224 | bytes 11010048 | tf_op jit(solution)/shard_map/dot_general | solution.py:573
  277.6 2.1 convert_element_type.30
  279.7 69.6 %reduce-scatter.5.cloned.1.call-done = f32[64,4096]{1,0:T(8,128)} async-done(((f32[1024,4096]{1,0:T(8,128)}), f32[64,4096]{1,0:T(8,128)}) %reduce-scatter.5.cloned.1.call-update) | async-done | bytes 1048592 | tf_op jit(solution)/shard_map/reduce_scatter | solution.py:570
  349.3 2.1 convert_element_type.31
  (24 shorter events, 1.7 us)
Async XLA Ops:
  7.2 142.4 %all-gather.2.cloned.1.call-start = ((), (), s32[]{:S(2)}) async-start(), calls=%async_computation.2 | async-start | bytes 8912896 | tf_op jit(solution)/shard_map/all_gather | solution.py:519
  58.8 218.8 %reduce-scatter.3.cloned.1.call-start = ((), (), s32[]{:S(2)}) async-start(), calls=%async_computation.3 | async-start | bytes 5242880 | tf_op jit(solution)/shard_map/reduce_scatter | solution.py:556
  58.9 7.3 %copy-start.1 = (bf16[4096,2,128]{2,1,0:T(2,128)(2,1)S(1)}, bf16[4096,2,128]{2,1,0:T(2,128)(2,1)}, u32[]{:S(2)}) copy-start(bf16[4096,2,128]{2,1,0:T(2,128)(2,1)} %param.9) | copy-start | bytes 6291460
  58.9 7.3 %copy-start.2 = (bf16[4096,2,128]{2,1,0:T(2,128)(2,1)S(1)}, bf16[4096,2,128]{2,1,0:T(2,128)(2,1)}, u32[]{:S(2)}) copy-start(bf16[4096,2,128]{2,1,0:T(2,128)(2,1)} %param.8) | copy-start | bytes 6291460
  66.1 3.4 copy-start
  143.1 1.6 copy-start.4
  145.0 4.6 %copy-start.5 = (bf16[2,128,4096]{2,1,0:T(8,128)(2,1)S(1)}, bf16[2,128,4096]{2,1,0:T(8,128)(2,1)}, u32[]{:S(2)}) copy-start(bf16[2,128,4096]{2,1,0:T(8,128)(2,1)} %param.10) | copy-start | bytes 6291460
  176.1 173.2 %reduce-scatter.5.cloned.1.call-start = ((), (), s32[]{:S(2)}) async-start(), calls=%async_computation.4 | async-start | bytes 17825792 | tf_op jit(solution)/shard_map/reduce_scatter | solution.py:570
  240.7 1.0 copy-start.7
  247.5 3.8 %copy-start.6 = (bf16[2,512,512]{2,1,0:T(8,128)(2,1)S(1)}, bf16[2,512,512]{2,1,0:T(8,128)(2,1)}, u32[]{:S(2)}) copy-start(bf16[2,512,512]{2,1,0:T(8,128)(2,1)} %get-tuple-element.40) | copy-start | bytes 3145732
  266.7 3.8 %copy-start.3 = (bf16[2,512,256]{2,1,0:T(8,128)(2,1)S(1)}, bf16[2,512,256]{2,1,0:T(8,128)(2,1)}, u32[]{:S(2)}) copy-start(bf16[2,512,256]{2,1,0:T(8,128)(2,1)} %get-tuple-element.25) | copy-start | bytes 1572868
Sparse Core Ops, SparseCore 0:
  58.9 90.5 all-gather.1
  176.2 45.9 reduce-scatter.2
  240.8 108.4 reduce-scatter.4

commit v4 on v3

--- a/solution.py
+++ b/solution.py
@@ -162,7 +162,8 @@
     own = pltpu.make_async_copy(kv_ref, kv_buf.at[pl.ds(2 * rank, 2)], sems.at[0])
     own.start()
     own.wait()
-    for half in range(2):
+
+    def diagonal(half, carry):
         for h in range(heads):
             cols = slice(h * dim, (h + 1) * dim)
             vcols = slice(width + h * dim, width + (h + 1) * dim)
@@ -175,6 +176,9 @@
             m_ref[half, h] = jnp.broadcast_to(m, (half_rows, dim))
             l_ref[half, h] = jnp.broadcast_to(jnp.sum(p, axis=1, keepdims=True), (half_rows, dim))
             acc_ref[half, h] = dot_n(p.astype(BF16), v_blk)
+        return carry
+
+    lax.fori_loop(0, 2, diagonal, 0)
 
     def unit(late, slot):
         for h in range(heads):
@@ -191,8 +195,11 @@
             l_ref[late, h] = l_ref[late, h] * factor + jnp.sum(p, axis=1, keepdims=True)
             acc_ref[late, h] = acc_ref[late, h] * factor + dot_n(p.astype(BF16), v_blk)
 
-    def visit(first, count, shard_of):
-        def step(t, carry):
+    def visit_all(count, shard_of, actions):
+        def step(u, carry):
+            for pos, action in actions.items():
+                pl.when(u == pos)(action)
+            t = u + (u > 0).astype(jnp.int32)
             shard = shard_of(t // 2)
             after = (shard > rank).astype(jnp.int32)
             second = lax.rem(t, 2)
@@ -200,7 +207,7 @@
             slot = 2 * shard + jnp.where(second == 1, after, 0)
             unit(late, slot)
             return carry
-        lax.fori_loop(first, first + count, step, 0)
+        lax.fori_loop(0, count, step, 0)
 
     offsets = [(0, 0), (0, 1), (n_x - 1, 0), (1, 0), (n_x - 1, 1), (1, 1), (2, 0), (2, 1)]
 
@@ -210,36 +217,43 @@
             out = jnp.where(idx == pos, rank_of(*offsets[pos]), out)
         return out
 
-    visit(0, 1, shard_of)
-    wait_recv("own_x")
-    visit(2, 2, shard_of)
-    wait_recv("prev")
-    start("far_lo", "prev_x")
-    wait_recv("next")
-    start("far_hi", "next_x")
-    visit(4, 4, shard_of)
-    w_wait("prev")
-    w_start("far_lo", "prev_x")
-    w_wait("next")
-    w_start("far_hi", "next_x")
-    wait_recv("prev_x", "next_x")
-    visit(8, 2, shard_of)
-    wait_recv("far_lo", "far_hi")
-    start("far_lo_x", "far_hi_x")
-    visit(10, 4, shard_of)
-    wait_recv("far_lo_x", "far_hi_x")
     out = pltpu.make_async_copy(kv_buf, all_ref, sems.at[0])
-    out.start()
-    visit(14, 2, shard_of)
+
+    def take_near():
+        wait_recv("prev")
+        start("far_lo", "prev_x")
+        wait_recv("next")
+        start("far_hi", "next_x")
+
+    def take_near_other():
+        w_wait("prev")
+        w_start("far_lo", "prev_x")
+        w_wait("next")
+        w_start("far_hi", "next_x")
+        wait_recv("prev_x", "next_x")
+
+    def take_far():
+        wait_recv("far_lo", "far_hi")
+        start("far_lo_x", "far_hi_x")
+
+    def take_far_other():
+        wait_recv("far_lo_x", "far_hi_x")
+        out.start()
+
+    visit_all(2 * n_sh - 1, shard_of, {1: lambda: wait_recv("own_x"), 3: take_near, 7: take_near_other, 9: take_far, 13: take_far_other})
     w_wait("far_lo", "far_hi")
     w_start("far_lo_x", "far_hi_x")
-    for half in range(2):
+
+    def finish(half, carry):
         for h in range(heads):
             cols = slice(h * dim, (h + 1) * dim)
             l = l_ref[half, h]
             o_ref[half, :, cols] = (acc_ref[half, h] / l).astype(BF16)
             lse = m_ref[half, h] * log2e_scale + jnp.log2(l)
             lse_ref[half, h:h + 1, :] = jnp.transpose(lse)[:1]
+        return carry
+
+    lax.fori_loop(0, 2, finish, 0)
     out.wait()
     own_w.wait()
     w_wait("prev_x", "next_x", "far_lo_x", "far_hi_x")
@@ -297,10 +311,14 @@
     half_rows = q_ref.shape[1]
     scale = dim ** -0.5
     log2e_scale = math.log2(math.e) * scale
-    for half in range(2):
+
+    def spread(half, carry):
         for h in range(heads):
             lse_ref[half, h] = jnp.transpose(jnp.broadcast_to(st_ref[half, h:h + 1, :], (dim, half_rows)))
             dot_ref[half, h] = jnp.transpose(jnp.broadcast_to(st_ref[half, heads + h:heads + h + 1, :], (dim, half_rows)))
+        return carry
+
+    lax.fori_loop(0, 2, spread, 0)
     for copy in load:
         copy.wait()
 
@@ -317,9 +335,12 @@
         ds = (p * (dp - dot_ref[half, h][:, :1])).astype(BF16)
         return dot_n(ds, k_blk)
 
-    for half in range(2):
+    def query_diagonal(half, carry):
         for h in range(heads):
             acc_ref[half, h] = query_part(half, 2 * rank + half, h, True)
+        return carry
+
+    lax.fori_loop(0, 2, query_diagonal, 0)
 
     def query_step(t, carry):
         late = (t >= rank).astype(jnp.int32)
@@ -351,14 +372,20 @@
         ds = (p * (dp - st_buf[slot, heads + h:heads + h + 1, :])).astype(BF16)
         return dot_n(ds, q_blk), dot_n(p.astype(BF16), do_blk)
 
-    for half in range(2):
+    def key_diagonal(half, carry):
         for h in range(heads):
             dk_acc[half, h], dv_acc[half, h] = key_part(half, 2 * rank + half, h, True)
+        return carry
+
+    lax.fori_loop(0, 2, key_diagonal, 0)
 
     offsets = [(0, 0), (0, 1), (n_x - 1, 0), (1, 0), (n_x - 1, 1), (1, 1), (2, 0), (2, 1)]
 
-    def visit(first, count):
-        def step(t, carry):
+    def visit_all(count, actions):
+        def step(u, carry):
+            for at_step, action in actions.items():
+                pl.when(u == at_step)(action)
+            t = u + (u > 0).astype(jnp.int32)
             idx = t // 2
             shard = rank_of(*offsets[0])
             for pos in range(1, n_sh):
@@ -372,18 +399,14 @@
                 dk_acc[late, h] = dk_acc[late, h] + dk_part
                 dv_acc[late, h] = dv_acc[late, h] + dv_part
             return carry
-        lax.fori_loop(first, first + count, step, 0)
-
-    visit(0, 1)
-    wait_recv("own_x")
-    visit(2, 6)
-    wait_recv("prev_x", "next_x")
-    visit(8, 2)
-    wait_recv("far_lo", "far_hi")
-    start("far_lo_x", "far_hi_x")
-    visit(10, 4)
-    wait_recv("far_lo_x", "far_hi_x")
-    visit(14, 2)
+        lax.fori_loop(0, count, step, 0)
+
+    def take_far():
+        wait_recv("far_lo", "far_hi")
+        start("far_lo_x", "far_hi_x")
+
+    visit_all(2 * n_sh - 1, {1: lambda: wait_recv("own_x"), 7: lambda: wait_recv("prev_x", "next_x"), 9: take_far,
+                             13: lambda: wait_recv("far_lo_x", "far_hi_x")})
     for half in range(2):
         for h in range(heads):
             cols = slice(h * dim, (h + 1) * dim)

time: 364 us -> 359 us (0.986); the launches traced: 358 us -> 359 us
  transfers between devices with their start and end apart: 3 -> 3, of which waited for: 2 -> 2; matrix products, arithmetic and copies ran while one was open for 19% -> 19% of each run, Pallas kernels for 33% -> 34%
where the time goes in v4:
time: 359 us
  Pallas kernels  184 us (51%)
  waiting for transfers between devices  71.1 us (20%)
  matrix products  64.1 us (18%)
  local copies, waits for them, and re-layouts  17.8 us (5%)
  between operations  13.9 us (4%)
  other arithmetic  7.06 us (2%)
    reduce_scatter x1, waiting for transfers between devices, device_fn(): lax.psum_scatter(dx_part, 'tp', scatter_dimension=0, tiled=True)  69.4 us
    pallas_call x1, Pallas kernels, device_fn(): attention_call(functools.partial(forward_kernel, n_sh, heads, dim), 'attn...  68.1 us
    pallas_call x1, Pallas kernels, device_fn(): attention_call(functools.partial(backward_kernel, n_sh, heads, dim), 'att...  52.6 us
    pallas_call x1, Pallas kernels, gather_rows(): pl.pallas_call(gather_rows_kernel, name='gather_rows', out_shape=jax.Shap...  51.6 us
    dot_general x4, matrix products, weight_grad(): lax.dot_general(lhs, rhs, ROWS_CONTRACT, preferred_element_type=F32)  24.5 us
    dot_general x3, matrix products, dot_n(): return jnp.dot(lhs, rhs, preferred_element_type=F32)  20.6 us
    dot_general x2, matrix products, dot_t(): return lax.dot_general(lhs, rhs, COLS_CONTRACT, preferred_element_type=F32)  19 us
    unnamed x22, local copies, waits for them, and re-layouts  17.2 us
  transfers between devices with their start and end apart: 3, of which 2 were waited for; matrix products, arithmetic and copies ran while one was open for 19% of the time, Pallas kernels for 34%

profile of v4, /device:TPU:0, one launch (start us, length us, event | category | flops | bytes accessed | tf_op | source)
XLA Modules:
  0.0 358.5 jit_solution(9178733986794991282)
XLA Ops:
  7.2 51.6 %gather_rows.1 = bf16[16,64,4096]{2,1,0:T(8,128)(2,1)} custom-call(bf16[64,4096]{1,0:T(8,128)(2,1)} %x_ref.1), custom_call_target="tpu_custom_call" | custom-call | tf_op jit(solution)/shard_map/gather_rows/pallas_call | solution.py:501
  58.9 7.3 %fusion.14 = bf16[1024,256]{1,0:T(8,128)(2,1)} fusion(bf16[1024,4096]{1,0:T(8,128)(2,1)} %bitcast.52, bf16[512,8,2,128]{3,2,1,0:T(2,128)(2,1)} %bitcast.67), kind=kOutput, calls=%fused_computation.22 | convolution fusion | flops 2147745792 | bytes 11010048 | tf_op jit(solution)/shard_map/dot_general | solution.py:28
  66.8 2.7 copy-done
  69.5 5.5 %fusion.11 = bf16[1024,512]{1,0:T(8,128)(2,1)} fusion(bf16[1024,4096]{1,0:T(8,128)(2,1)S(1)} %bitcast.56, bf16[4096,256]{1,0:T(8,128)(2,1)S(1)} %get-tuple-element.48, bf16[4096,256]{1,0:T(8,128)(2,1)S(1)} %get-tuple-element.49), kind=kOutput, calls=%fused_computation.21 | convolution fusion | flops 4303880192 | bytes 13631488 | tf_op jit(solution)/shard_map/dot_general | solution.py:28
  75.0 68.1 %attn_fwd.1 = (bf16[2,512,256]{2,1,0:T(8,128)(2,1)}, f32[2,2,512]{2,1,0:T(2,128)}, bf16[16,512,512]{2,1,0:T(8,128)(2,1)}, bf16[4,256,4096]{2,1,0:T(8,128)(2,1)}) custom-call(bf16[2,512,256]{2,1,0:T(8,128)(2,1)} %bitcast.82, bf16[2,512,512]{2,1,0:T(8,128)(2,1)} %bitcast.81, bf16[256,4096]{1,0:T(8,128)(2,1)} %bitcast.74), custom_call_target="tpu_custom_call" | custom-call | flops 9126805504 | bytes 10485760 | tf_op jit(solution)/shard_map/attn_fwd/pallas_call | solution.py:553
  143.7 1.0 copy-done.4
  145.0 2.9 pad_maximum_fusion
  147.9 1.7 all-gather.2.cloned.1.call-done
  149.6 6.5 %convolution_convert_fusion.4 = bf16[1024,256]{1,0:T(8,128)(2,1)} fusion(bf16[1024,4096]{1,0:T(8,128)(2,1)} %all-gather.2.cloned.1.call-done, bf16[256,4096]{1,0:T(8,128)(2,1)S(1)} %bitcast.75), kind=kOutput, calls=%fused_computation.23 | convolution fusion | flops 2147745792 | bytes 11010048 | tf_op jit(solution)/shard_map/dot_general | solution.py:24
  156.1 12.1 %attn_stats.1 = (f32[2,8,512]{2,1,0:T(8,128)}, bf16[4,64,1024]{2,1,0:T(8,128)(2,1)}) custom-call(bf16[4,4,64,256]{3,2,1,0:T(8,128)(2,1)} %bitcast.64, bf16[2,512,256]{2,1,0:T(8,128)(2,1)} %bitcast.72, f32[2,2,512]{2,1,0:T(2,128)} %get-tuple-element.32.lse_ref), custom_call_target="tpu_custom_call" | custom-call | tf_op jit(solution)/shard_map/attn_stats/pallas_call | solution.py:567
  168.2 7.9 %fusion.21 = f32[256,4096]{1,0:T(8,128)} fusion(bf16[256,1024]{1,0:T(8,128)(2,1)} %bitcast.76, bf16[1024,4096]{1,0:T(8,128)(2,1)} %bitcast.77), kind=kOutput, calls=%fused_computation.28 | convolution fusion | flops 2147483648 | bytes 13107200 | tf_op jit(solution)/shard_map/dot_general | solution.py:28
  176.2 52.6 %attn_bwd.1 = (bf16[2,512,256]{2,1,0:T(8,128)(2,1)}, bf16[2,512,512]{2,1,0:T(8,128)(2,1)}) custom-call(bf16[2,512,256]{2,1,0:T(8,128)(2,1)} %bitcast.83, bf16[2,512,256]{2,1,0:T(8,128)(2,1)} %bitcast.73, f32[2,8,512]{2,1,0:T(8,128)} %get-tuple-element.37.st_ref, bf16[16,512,512]{2,1,0:T(8,128)(2,1)} %get-tuple-element.38.all_ref), custom_call_target="tpu_custom_call" | custom-call | flops 15971909632 | bytes 10485760 | tf_op jit(solution)/shard_map/attn_bwd/pallas_call | solution.py:581
  228.8 12.5 %fusion.7 = f32[1024,4096]{1,0:T(8,128)} fusion(bf16[4096,768]{1,0:T(8,128)(2,1)} %pad_maximum_fusion, bf16[1024,512]{1,0:T(8,128)(2,1)} %bitcast.78, bf16[1024,256]{1,0:T(8,128)(2,1)} %bitcast.84), kind=kOutput, calls=%fused_computation.17 | convolution fusion | flops 6445596672 | bytes 24641536 | tf_op jit(solution)/shard_map/dot_general | solution.py:24
  241.3 1.0 copy-done.7
  242.4 5.8 %convolution_convert_fusion.3 = bf16[4096,256]{0,1:T(8,128)(2,1)S(1)} fusion(bf16[1024,4096]{1,0:T(8,128)(2,1)} %bitcast.53, bf16[1024,256]{1,0:T(8,128)(2,1)S(1)} %bitcast.85), kind=kOutput, calls=%fused_computation.4 | convolution fusion | flops 2148532224 | bytes 11010048 | tf_op jit(solution)/shard_map/dot_general | solution.py:596
  248.2 3.8 %copy.12 = bf16[1,4096,2,128]{3,2,1,0:T(2,128)(2,1)} copy(bf16[1,4096,2,128]{1,3,2,0:T(8,128)(2,1)S(1)} %bitcast.70) | data formatting | bytes 4194304
  251.9 5.8 %convolution_convert_fusion.2 = bf16[4096,256]{0,1:T(8,128)(2,1)S(1)} fusion(bf16[1024,4096]{1,0:T(8,128)(2,1)} %bitcast.54, bf16[1024,512]{1,0:T(8,128)(2,1)S(1)} %bitcast.80), kind=kOutput, calls=%fused_computation.3 | convolution fusion | flops 2148532224 | bytes 11010048 | tf_op jit(solution)/shard_map/dot_general | solution.py:596
  257.7 4.0 %copy.13 = bf16[1,4096,2,128]{3,2,1,0:T(2,128)(2,1)} copy(bf16[1,4096,2,128]{1,3,2,0:T(8,128)(2,1)S(1)} %bitcast.71) | data formatting | bytes 4194304
  261.8 5.8 %convolution_convert_fusion.1 = bf16[4096,256]{0,1:T(8,128)(2,1)S(1)} fusion(bf16[1024,4096]{1,0:T(8,128)(2,1)} %bitcast.55, bf16[1024,512]{1,0:T(8,128)(2,1)} %bitcast.79), kind=kOutput, calls=%fused_computation.2 | convolution fusion | flops 2148532224 | bytes 11010048 | tf_op jit(solution)/shard_map/dot_general | solution.py:596
  267.6 3.8 %copy.14 = bf16[1,4096,2,128]{3,2,1,0:T(2,128)(2,1)} copy(bf16[1,4096,2,128]{1,3,2,0:T(8,128)(2,1)S(1)} %bitcast.69) | data formatting | bytes 4194304
  271.4 7.1 %convolution_convert_fusion = bf16[256,4096]{1,0:T(8,128)(2,1)} fusion(bf16[1024,256]{1,0:T(8,128)(2,1)S(1)} %bitcast.65, bf16[1024,4096]{1,0:T(8,128)(2,1)} %all-gather.2.cloned.1.call-done), kind=kOutput, calls=%fused_computation.1 | convolution fusion | flops 2148532224 | bytes 11010048 | tf_op jit(solution)/shard_map/dot_general | solution.py:596
  278.5 2.1 convert_element_type.30
  280.6 69.4 %reduce-scatter.5.cloned.1.call-done = f32[64,4096]{1,0:T(8,128)} async-done(((f32[1024,4096]{1,0:T(8,128)}), f32[64,4096]{1,0:T(8,128)}) %reduce-scatter.5.cloned.1.call-update) | async-done | bytes 1048592 | tf_op jit(solution)/shard_map/reduce_scatter | solution.py:593
  349.9 2.1 convert_element_type.31
  (24 shorter events, 1.7 us)
Async XLA Ops:
  7.2 142.4 %all-gather.2.cloned.1.call-start = ((), (), s32[]{:S(2)}) async-start(), calls=%async_computation.2 | async-start | bytes 8912896 | tf_op jit(solution)/shard_map/all_gather | solution.py:542
  58.8 219.7 %reduce-scatter.3.cloned.1.call-start = ((), (), s32[]{:S(2)}) async-start(), calls=%async_computation.3 | async-start | bytes 5242880 | tf_op jit(solution)/shard_map/reduce_scatter | solution.py:579
  58.9 7.3 %copy-start.1 = (bf16[4096,2,128]{2,1,0:T(2,128)(2,1)S(1)}, bf16[4096,2,128]{2,1,0:T(2,128)(2,1)}, u32[]{:S(2)}) copy-start(bf16[4096,2,128]{2,1,0:T(2,128)(2,1)} %param.9) | copy-start | bytes 6291460
  58.9 7.3 %copy-start.2 = (bf16[4096,2,128]{2,1,0:T(2,128)(2,1)S(1)}, bf16[4096,2,128]{2,1,0:T(2,128)(2,1)}, u32[]{:S(2)}) copy-start(bf16[4096,2,128]{2,1,0:T(2,128)(2,1)} %param.8) | copy-start | bytes 6291460
  66.1 3.4 copy-start
  143.1 1.6 copy-start.4
  145.0 4.6 %copy-start.5 = (bf16[2,128,4096]{2,1,0:T(8,128)(2,1)S(1)}, bf16[2,128,4096]{2,1,0:T(8,128)(2,1)}, u32[]{:S(2)}) copy-start(bf16[2,128,4096]{2,1,0:T(8,128)(2,1)} %param.10) | copy-start | bytes 6291460
  176.1 173.8 %reduce-scatter.5.cloned.1.call-start = ((), (), s32[]{:S(2)}) async-start(), calls=%async_computation.4 | async-start | bytes 17825792 | tf_op jit(solution)/shard_map/reduce_scatter | solution.py:593
  241.3 1.0 copy-start.7
  248.2 3.8 %copy-start.6 = (bf16[2,512,512]{2,1,0:T(8,128)(2,1)S(1)}, bf16[2,512,512]{2,1,0:T(8,128)(2,1)}, u32[]{:S(2)}) copy-start(bf16[2,512,512]{2,1,0:T(8,128)(2,1)} %get-tuple-element.40) | copy-start | bytes 3145732
  267.6 3.8 %copy-start.3 = (bf16[2,512,256]{2,1,0:T(8,128)(2,1)S(1)}, bf16[2,512,256]{2,1,0:T(8,128)(2,1)}, u32[]{:S(2)}) copy-start(bf16[2,512,256]{2,1,0:T(8,128)(2,1)} %get-tuple-element.25) | copy-start | bytes 1572868
Sparse Core Ops, SparseCore 0:
  58.9 90.5 all-gather.1
  176.3 45.9 reduce-scatter.2
  241.5 108.4 reduce-scatter.4
